TPU v7x, 32 devices: a whole 2x2x4 slice. The times are simulated.
32 devices in a mesh: dp: 4 (over y, core), cp: 8 (over z, x).
Axes of the slice: x: 2, y: 2, z: 4, core: 2. Of those that a mesh axis runs over, the one named last changes fastest.
Arguments:
- tokens: bfloat16 [8192, 1600], P(('dp', 'cp')), may hold values from -6 to 6
- params: bfloat16 [19456, 1600], P(('dp', 'cp')), as said below
- out_grad: bfloat16 [8192, 1600], P(('dp', 'cp')), may hold values from -6 to 6
- lengths: int32 [4, 2], P('dp'), may hold values from 1024 to 1024, as said below
Outputs:
- output: bfloat16 [8192, 1600], P(('dp', 'cp'))
- input_grad: bfloat16 [8192, 1600], P(('dp', 'cp'))
- param_grad: float32 [19456, 1600], P(('dp', 'cp'))
Inputs may be any that keep to these rules, and one draw needn't show every extreme that they name: Rows of params past the used ones are never read. Multiples of 128; a group's lengths sum to 2048; one of them is 1024 and one 1024.
All inputs are finite; a program needn't handle non-finite values.
Results may differ from a plain program's by a relative error of at most 0.028.
Values may be sent and summed in bfloat16 or wider, within the bound.
A program may use at most 832 MiB of HBM per device.

v0:
```python
import jax
import jax.numpy as jnp
from jax import lax
from jax.sharding import PartitionSpec as P

HEADS = 25
FF = 6400
HEAD_DIM = 64
TILE = 128
MIN_LEN = 1024
MAX_LEN = 4096


EPSILON = 1e-05
MASKED = -1e30
GELU_SCALE = 0.7978845608028654


def from_behind(value, axis, by):
    length = lax.axis_size(axis)
    pairs = [(i, i + by) for i in range(length) if 0 <= i + by < length]
    return lax.ppermute(value, axis, pairs)


def layer_norm(values, gain_row, bias_row):
    centre = values - jnp.mean(values, axis=-1, keepdims=True)
    spread = jnp.mean(centre * centre, axis=-1, keepdims=True)
    return centre * lax.rsqrt(spread + EPSILON) * gain_row + bias_row


def gelu_tanh(values):
    return (
        0.5 * values * (1.0 + jnp.tanh(GELU_SCALE * (values + 0.044715 * values * values * values)))
    )


def segment_of(position, seq_ends):
    return jnp.sum((position[:, None] >= seq_ends[None, :]).astype(jnp.int32), axis=1)


def unpack(gathered, model_width, hidden):
    out_end = 4 * model_width
    fc_end = out_end + hidden
    proj_end = fc_end + hidden
    vec_end = proj_end + 8
    return (
        gathered[0 : 3 * model_width],
        gathered[3 * model_width : out_end],
        gathered[out_end:fc_end],
        gathered[fc_end:proj_end],
        gathered[proj_end:vec_end].astype(jnp.float32),
        gathered[vec_end : vec_end + hidden // model_width].astype(jnp.float32).reshape(hidden),
    )


def matmul_nt(left_mat, right_mat):
    return lax.dot_general(
        left_mat, right_mat, (((1,), (1,)), ((), ())), preferred_element_type=jnp.float32
    )


def matmul_tn(left_mat, right_mat):
    return lax.dot_general(
        left_mat, right_mat, (((0,), (0,)), ((), ())), preferred_element_type=jnp.float32
    )


def matmul_nn(left_mat, right_mat):
    return jnp.dot(left_mat, right_mat, preferred_element_type=jnp.float32)


def per_device(tokens, params, out_grad, lengths):
    tok_rows, model_width = tokens.shape
    hidden = FF
    head_count = HEADS
    head_size = HEAD_DIM
    cp_count = lax.axis_size("cp")
    group_rows = tok_rows * cp_count
    seq_count = lengths.shape[1]
    longest = min(MAX_LEN, group_rows - (seq_count - 1) * MIN_LEN)
    reach_back = min(cp_count - 1, (longest + tok_rows - TILE - 1) // tok_rows)
    pair_count = (reach_back + 2) // 2
    score_scale = head_size ** (-0.5)
    gathered = lax.all_gather(params, ("dp", "cp"), axis=0, tiled=True)
    w_attn, w_out, w_fc, w_proj, vectors, fc_bias = unpack(gathered, model_width, hidden)
    inputs = tokens.astype(jnp.float32)
    act_one = layer_norm(inputs, vectors[0], vectors[1]).astype(jnp.bfloat16)
    qkv_bias = jnp.concatenate([vectors[2], jnp.zeros_like(vectors[2]), vectors[3]])
    qkv = (matmul_nt(act_one, w_attn) + qkv_bias).astype(jnp.bfloat16)
    queries = qkv[:, :model_width].reshape(tok_rows, head_count, head_size)
    key_value = qkv[:, model_width:]
    device = lax.axis_index("cp")
    seq_ends = jnp.cumsum(lengths[0])
    query_pos = device * tok_rows + jnp.arange(tok_rows, dtype=jnp.int32)
    query_seg = segment_of(query_pos, seq_ends)
    store = jnp.zeros((2 * pair_count, tok_rows, 2 * model_width), jnp.bfloat16)
    store = store.at[0].set(key_value)

    def fetch(step_index, state_pair):
        moving, held_rows = state_pair
        moving = from_behind(moving, "cp", 1)
        return (moving, lax.dynamic_update_index_in_dim(held_rows, moving, step_index, 0))

    _, store = lax.fori_loop(1, reach_back + 1, fetch, (key_value, store))

    def pair_mask(pair_index):
        owners = 2 * pair_index + jnp.arange(2, dtype=jnp.int32)
        key_pos = (
            (device - owners)[:, None] * tok_rows + jnp.arange(tok_rows, dtype=jnp.int32)[None, :]
        ).reshape(2 * tok_rows)
        usable = jnp.broadcast_to((owners <= reach_back)[:, None], (2, tok_rows)).reshape(
            2 * tok_rows
        ) & (key_pos >= 0)
        key_seg = segment_of(key_pos, seq_ends)
        return (
            (key_seg[None, :] == query_seg[:, None])
            & (key_pos[None, :] <= query_pos[:, None])
            & usable[None, :]
        )

    def pair_rows(pair_index):
        block_rows = lax.dynamic_slice_in_dim(store, 2 * pair_index, 2, 0).reshape(
            2 * tok_rows, 2 * model_width
        )
        return (
            block_rows[:, :model_width].reshape(2 * tok_rows, head_count, head_size),
            block_rows[:, model_width:].reshape(2 * tok_rows, head_count, head_size),
        )

    def pair_scores(key_rows, allowed):
        raw_scores = (
            jnp.einsum("qhd,khd->hqk", queries, key_rows, preferred_element_type=jnp.float32)
            * score_scale
        )
        return jnp.where(allowed[None], raw_scores, MASKED)

    def visit(work):

        def step_pair(pair_index, running):
            allowed = pair_mask(pair_index)
            result = work(pair_index, allowed, running)
            return result

        return step_pair

    def add_total(pair_index, allowed, running):
        row_top, summed = running
        key_rows, _ = pair_rows(pair_index)
        scores = pair_scores(key_rows, allowed)
        new_top = jnp.maximum(row_top, jnp.max(scores, axis=-1, keepdims=True))
        summed = summed * jnp.exp(row_top - new_top) + jnp.sum(
            jnp.exp(scores - new_top), axis=-1, keepdims=True
        )
        return (new_top, summed)

    start_top = jnp.full((head_count, tok_rows, 1), MASKED, jnp.float32)
    start_sum = jnp.zeros((head_count, tok_rows, 1), jnp.float32)
    row_top, summed = lax.fori_loop(0, pair_count, visit(add_total), (start_top, start_sum))
    log_total = row_top + jnp.log(summed)

    def add_mix(pair_index, allowed, running):
        key_rows, value_rows = pair_rows(pair_index)
        prob_rows = jnp.exp(pair_scores(key_rows, allowed) - log_total).astype(jnp.bfloat16)
        return running + jnp.einsum(
            "hqk,khd->qhd", prob_rows, value_rows, preferred_element_type=jnp.float32
        )

    mixed_full = lax.fori_loop(
        0, pair_count, visit(add_mix), jnp.zeros((tok_rows, head_count, head_size), jnp.float32)
    )
    mixed = mixed_full.reshape(tok_rows, model_width).astype(jnp.bfloat16)
    attn_out = matmul_nt(mixed, w_out) + vectors[4]
    residual = inputs + attn_out
    act_two = layer_norm(residual, vectors[5], vectors[6]).astype(jnp.bfloat16)
    pre_act = matmul_nt(act_two, w_fc) + fc_bias
    act_hidden = gelu_tanh(pre_act).astype(jnp.bfloat16)
    output = (residual + matmul_nn(act_hidden, w_proj) + vectors[7]).astype(jnp.bfloat16)
    gathered = lax.all_gather(params, ("dp", "cp"), axis=0, tiled=True)
    w_attn, w_out, w_fc, w_proj, vectors, fc_bias = unpack(gathered, model_width, hidden)
    grad_out_f = out_grad.astype(jnp.float32)
    grad_hidden = matmul_nt(out_grad, w_proj)
    _, pull_gelu = jax.vjp(gelu_tanh, pre_act)
    grad_fc = pull_gelu(grad_hidden)[0].astype(jnp.bfloat16)
    grad_act_two = matmul_nn(grad_fc, w_fc)
    _, pull_two = jax.vjp(layer_norm, residual, vectors[5], vectors[6])
    grad_res_norm, grad_gain_two, grad_bias_two = pull_two(grad_act_two)
    grad_res = grad_out_f + grad_res_norm
    grad_attn = grad_res.astype(jnp.bfloat16)
    grad_mix = (
        matmul_nn(grad_attn, w_out).astype(jnp.bfloat16).reshape(tok_rows, head_count, head_size)
    )
    grad_dot = jnp.transpose(jnp.sum(grad_mix.astype(jnp.float32) * mixed_full, axis=-1), (1, 0))[
        :, :, None
    ]

    def add_grads(pair_index, allowed, running):
        grad_query, grad_store = running
        key_rows, value_rows = pair_rows(pair_index)
        prob_rows = jnp.exp(pair_scores(key_rows, allowed) - log_total)
        grad_probs = jnp.einsum(
            "qhd,khd->hqk", grad_mix, value_rows, preferred_element_type=jnp.float32
        )
        grad_scores = (prob_rows * (grad_probs - grad_dot)).astype(jnp.bfloat16)
        grad_query = (
            grad_query
            + jnp.einsum("hqk,khd->qhd", grad_scores, key_rows, preferred_element_type=jnp.float32)
            * score_scale
        )
        grad_keys = (
            jnp.einsum("hqk,qhd->khd", grad_scores, queries, preferred_element_type=jnp.float32)
            * score_scale
        )
        grad_values = jnp.einsum(
            "hqk,qhd->khd",
            prob_rows.astype(jnp.bfloat16),
            grad_mix,
            preferred_element_type=jnp.float32,
        )
        pair_grad = jnp.concatenate(
            [
                grad_keys.reshape(2 * tok_rows, model_width),
                grad_values.reshape(2 * tok_rows, model_width),
            ],
            axis=1,
        )
        pair_grad = pair_grad.reshape(2, tok_rows, 2 * model_width)
        grad_store = lax.dynamic_update_slice_in_dim(grad_store, pair_grad, 2 * pair_index, 0)
        return (grad_query, grad_store)

    start_query = jnp.zeros((tok_rows, head_count, head_size), jnp.float32)
    start_store = jnp.zeros((2 * pair_count, tok_rows, 2 * model_width), jnp.float32)
    grad_query, grad_store = lax.fori_loop(
        0, pair_count, visit(add_grads), (start_query, start_store)
    )

    def send_back(step_index, moving):
        moving = moving + lax.dynamic_index_in_dim(
            grad_store, reach_back - step_index, 0, keepdims=False
        )
        return from_behind(moving.astype(jnp.bfloat16), "cp", -1).astype(moving.dtype)

    returned = lax.fori_loop(
        0, reach_back, send_back, jnp.zeros((tok_rows, 2 * model_width), jnp.float32)
    )
    grad_kv = returned + grad_store[0]
    grad_qkv = jnp.concatenate([grad_query.reshape(tok_rows, model_width), grad_kv], axis=1).astype(
        jnp.bfloat16
    )
    grad_qkv_f = grad_qkv.astype(jnp.float32)
    grad_act_one = matmul_nn(grad_qkv, w_attn)
    _, pull_one = jax.vjp(layer_norm, inputs, vectors[0], vectors[1])
    grad_in_norm, grad_gain_one, grad_bias_one = pull_one(grad_act_one)
    input_grad = (grad_res + grad_in_norm).astype(jnp.bfloat16)
    grad_vectors = jnp.stack(
        [
            grad_gain_one,
            grad_bias_one,
            jnp.sum(grad_qkv_f[:, :model_width], axis=0),
            jnp.sum(grad_qkv_f[:, 2 * model_width :], axis=0),
            jnp.sum(grad_attn.astype(jnp.float32), axis=0),
            grad_gain_two,
            grad_bias_two,
            jnp.sum(grad_out_f, axis=0),
        ]
    )
    grad_fc_bias = jnp.sum(grad_fc.astype(jnp.float32), axis=0).reshape(
        hidden // model_width, model_width
    )
    used_rows = 4 * model_width + 2 * hidden + 8 + hidden // model_width
    total_rows = gathered.shape[0]
    local_grad = jnp.concatenate(
        [
            matmul_tn(grad_qkv, act_one),
            matmul_tn(grad_attn, mixed),
            matmul_tn(grad_fc, act_two),
            matmul_tn(act_hidden, out_grad),
            grad_vectors,
            grad_fc_bias,
            jnp.zeros((total_rows - used_rows, model_width), jnp.float32),
        ],
        axis=0,
    )
    dp_count = lax.axis_size("dp")
    device_count = dp_count * cp_count
    share_rows = total_rows // device_count
    spread_rows = local_grad.reshape(device_count, 1, share_rows, model_width)
    received = lax.all_to_all(
        spread_rows.astype(jnp.bfloat16), ("dp", "cp"), split_axis=0, concat_axis=1, tiled=True
    ).astype(spread_rows.dtype)
    param_grad = jnp.sum(received, axis=1).reshape(share_rows, model_width)
    return (output, input_grad, param_grad)


def solution(mesh):
    in_specs = (P(("dp", "cp"), None), P(("dp", "cp"), None), P(("dp", "cp"), None), P("dp", None))
    out_specs = (P(("dp", "cp"), None), P(("dp", "cp"), None), P(("dp", "cp"), None))
    return jax.shard_map(
        per_device, mesh=mesh, in_specs=in_specs, out_specs=out_specs, check_vma=False
    )
```

profile of v0, /device:TPU:10, one launch (start us, length us, event | category | flops | bytes accessed | tf_op | source)
XLA Modules:
  0.0 2929.8 jit_solution(15766116977980924574)
XLA Ops:
  11.1 343.3 %all-gather.2.cloned.1.call-done = bf16[19456,1600]{1,0:T(8,128)(2,1)} async-done(((bf16[608,1600]{1,0:T(8,128)(2,1)}), bf16[19456,1600]{1,0:T(8,128)(2,1)}) %all-gather.2.cloned.1.call-update) | async-done | bytes 62259216 | tf_op jit(solution)/shard_map/all_gather | solution.py:84
  379.1 168.2 %while.78 = (s32[]{:T(128)}, bf16[256,3200]{1,0:T(8,128)(2,1)}, bf16[6,256,3200]{2,1,0:T(8,128)(2,1)}, s32[]{:T(128)}, s32[]{:T(128)}, /*index=5*/s32[]{:T(128)}) while((s32[]{:T(128)}, bf16[256,3200]{1,0:T(8,128)(2,1)}, bf16[6,256,3200]{2,1,0:T(8,128)(2,1)}, s32[]{:T(128)}, s32[]{:T(128)}, /*index=5*/s32[]{:T(128)}) %tuple.201), condition=%wide.region_5.6_spmd, body=%wide.region_4.5_spmd.sunk | while | flops 5 | bytes 13107355 | solution.py:104
  383.7 35.8 %collective-permute-done = bf16[256,3200]{1,0:T(8,128)(2,1)S(1)} collective-permute-done((bf16[256,3200]{1,0:T(8,128)(2,1)}, bf16[256,3200]{1,0:T(8,128)(2,1)S(1)}, u32[]{:S(2)}, u32[]{:S(2)}) %collective-permute-start) | collective-permute-done | bytes 1638432 | tf_op jit(solution)/shard_map/while/body/eval_jaxpr/ppermute | solution.py:22
  427.2 34.9 %collective-permute-done = bf16[256,3200]{1,0:T(8,128)(2,1)S(1)} collective-permute-done((bf16[256,3200]{1,0:T(8,128)(2,1)}, bf16[256,3200]{1,0:T(8,128)(2,1)S(1)}, u32[]{:S(2)}, u32[]{:S(2)}) %collective-permute-start) | collective-permute-done | bytes 1638432 | tf_op jit(solution)/shard_map/while/body/eval_jaxpr/ppermute | solution.py:22
  469.8 34.0 %collective-permute-done = bf16[256,3200]{1,0:T(8,128)(2,1)S(1)} collective-permute-done((bf16[256,3200]{1,0:T(8,128)(2,1)}, bf16[256,3200]{1,0:T(8,128)(2,1)S(1)}, u32[]{:S(2)}, u32[]{:S(2)}) %collective-permute-start) | collective-permute-done | bytes 1638432 | tf_op jit(solution)/shard_map/while/body/eval_jaxpr/ppermute | solution.py:22
  511.5 33.3 %collective-permute-done = bf16[256,3200]{1,0:T(8,128)(2,1)S(1)} collective-permute-done((bf16[256,3200]{1,0:T(8,128)(2,1)}, bf16[256,3200]{1,0:T(8,128)(2,1)S(1)}, u32[]{:S(2)}, u32[]{:S(2)}) %collective-permute-start) | collective-permute-done | bytes 1638432 | tf_op jit(solution)/shard_map/while/body/eval_jaxpr/ppermute | solution.py:22
  547.3 17.6 copy.71
  564.9 70.1 %while.79 = (s32[]{:T(128)}, f32[25,256,1]{1,0,2:T(8,128)S(1)}, f32[25,256,1]{1,0,2:T(8,128)S(1)}, s32[]{:T(128)}, s32[2]{0:T(128)S(1)}, /*index=5*/s32[256]{0:T...) while((s32[]{:T(128)}, f32[25,256,1]{1,0,2:T(8,128)S(1)}, ...), condition=%wide.region_10.11_spmd.clone, body=%wide.region_6.0_spmd.clone.sunk | while | flops 442928640 | bytes 45804780 | solution.py:158
  635.0 52.8 %while.80 = (s32[]{:T(128)}, f32[256,25,64]{0,2,1:T(8,128)}, bf16[6,256,3200]{1,0,2:T(8,128)(2,1)}, s32[]{:T(128)}, s32[2]{0:T(128)S(1)}, /*index=5*/s32[256]{0:...) while((s32[]{:T(128)}, f32[256,25,64]{0,2,1:T(8,128)}, ...), condition=%wide.region_13.14_spmd.clone, body=%wide.region_11.13_spmd.clone.sunk | while | flops 853315840 | bytes 27344108 | solution.py:168
  695.8 13.8 fusion.40
  709.6 12.0 convolution_convert_fusion
  721.6 15.3 fusion.108
  736.9 12.1 convolution_convert_fusion.1
  749.0 17.1 multiply_reduce_fusion
  787.6 270.0 %while.81 = (s32[]{:T(128)}, f32[256,25,64]{0,2,1:T(8,128)}, f32[6,256,3200]{2,1,0:T(8,128)}, bf16[6,256,3200]{1,0,2:T(8,128)(2,1)}, s32[]{:T(128)}, /*index=5*/...) while((s32[]{:T(128)}, f32[256,25,64]{0,2,1:T(8,128)}, ...), condition=%wide.region_21.22_spmd.clone, body=%wide.region_19.21_spmd.clone.sunk | while | flops 2124304640 | bytes 214966704 | solution.py:232
  843.4 16.8 pad_maximum_fusion.5
  860.2 11.0 copy.129
  933.4 16.8 pad_maximum_fusion.5
  950.2 11.0 copy.129
  1023.4 16.8 pad_maximum_fusion.5
  1040.2 11.0 copy.129
  1057.6 165.3 %while.82 = (s32[]{:T(128)}, f32[256,3200]{1,0:T(8,128)}, f32[6,256,3200]{2,1,0:T(8,128)}, s32[]{:T(128)}, s32[]{:T(128)}, /*index=5*/s32[]{:T(128)}, s32[]{:T(128)}) while((s32[]{:T(128)}, f32[256,3200]{1,0:T(8,128)}, f32[6,256,3200]{2,1,0:T(8,128)}, s32[]{:T(128)}, s32[]{:T(128)}, /*index=5*/s32[]{:T(128)}, s32[]{:T(128)}) %tuple.213), condition=%wide.region_23.24_spmd.clone, body=%wide.region_22.23_spmd.clone.sunk | while | flops 3276807 | bytes 19660976 | solution.py:242
  1064.4 33.3 %collective-permute-done.1 = bf16[256,3200]{1,0:T(8,128)(2,1)S(1)} collective-permute-done((bf16[256,3200]{1,0:T(8,128)(2,1)S(1)}, bf16[256,3200]{1,0:T(8,128)(2,1)S(1)}, u32[]{:S(2)}, u32[]{:S(2)}) %collective-permute-start.1) | collective-permute-done | bytes 1638432 | tf_op jit(solution)/shard_map/while/body/eval_jaxpr/ppermute | solution.py:22
  1106.3 33.4 %collective-permute-done.1 = bf16[256,3200]{1,0:T(8,128)(2,1)S(1)} collective-permute-done((bf16[256,3200]{1,0:T(8,128)(2,1)S(1)}, bf16[256,3200]{1,0:T(8,128)(2,1)S(1)}, u32[]{:S(2)}, u32[]{:S(2)}) %collective-permute-start.1) | collective-permute-done | bytes 1638432 | tf_op jit(solution)/shard_map/while/body/eval_jaxpr/ppermute | solution.py:22
  1147.4 33.4 %collective-permute-done.1 = bf16[256,3200]{1,0:T(8,128)(2,1)S(1)} collective-permute-done((bf16[256,3200]{1,0:T(8,128)(2,1)S(1)}, bf16[256,3200]{1,0:T(8,128)(2,1)S(1)}, u32[]{:S(2)}, u32[]{:S(2)}) %collective-permute-start.1) | collective-permute-done | bytes 1638432 | tf_op jit(solution)/shard_map/while/body/eval_jaxpr/ppermute | solution.py:22
  1187.9 33.1 %collective-permute-done.1 = bf16[256,3200]{1,0:T(8,128)(2,1)S(1)} collective-permute-done((bf16[256,3200]{1,0:T(8,128)(2,1)S(1)}, bf16[256,3200]{1,0:T(8,128)(2,1)S(1)}, u32[]{:S(2)}, u32[]{:S(2)}) %collective-permute-start.1) | collective-permute-done | bytes 1638432 | tf_op jit(solution)/shard_map/while/body/eval_jaxpr/ppermute | solution.py:22
  1240.1 13.3 fusion.101
  1264.3 128.5 %concatenate.27 = bf16[19456,1600]{0,1:T(8,128)(2,1)} concatenate(bf16[4800,1600]{0,1:T(8,128)(2,1)} %convolution_convert_fusion.2, bf16[1600,1600]{0,1:T(8,128)(2,1)} %convolution_convert_fusion.3, bf16[6400,1600]{0,1:T(8,128)(2,1)} %convolution_convert_fusion.1, bf16[6400,1600]{0,1:T(8,128)(2,1)} %convolution_convert_fusion, bf16[1,1600]{0,1:T(8,128)(2,1)S(1)} %reshape.742, ...), dimensions={0} | concatenate | bytes 124518400 | tf_op jit(solution)/shard_map/concatenate | solution.py:271
  1392.8 78.5 %copy.85 = bf16[19456,1600]{1,0:T(8,128)(2,1)} copy(bf16[19456,1600]{0,1:T(8,128)(2,1)} %concatenate.27) | data formatting | bytes 124518400 | tf_op jit(solution)/shard_map/concatenate | solution.py:271
  1480.9 15.7 fusion.74
  1496.6 1403.7 %all-to-all-done = bf16[32,1,608,1600]{3,2,1,0:T(8,128)(2,1)} async-done(((bf16[32,1,608,1600]{3,2,1,0:T(8,128)(2,1)}), bf16[32,1,608,1600]{3,2,1,0:T(8,128)(2,1)}, u32[]{:S(2)}, u32[]{:S(2)}) %all-to-all-start) | async-done | bytes 62259232 | tf_op jit(solution)/shard_map/all_to_all | solution.py:287
  2900.3 22.4 convert_reduce_fusion
  (340 shorter events, 465.7 us)
Async XLA Ops:
  7.2 347.2 %all-gather.2.cloned.1.call-start = ((), (), s32[]{:S(2)}) async-start(), calls=%async_computation.1 | async-start | bytes 66772992 | tf_op jit(solution)/shard_map/all_gather | solution.py:84
  10.3 354.7 %copy-start.22 = (f32[256]{0:T(256)}, f32[256]{0:T(256)S(1)}, u32[]{:S(2)}) copy-start(f32[256]{0:T(256)S(1)} %broadcast_multiply_fusion.1) | copy-start | bytes 3076
  11.1 353.9 %copy-start.24 = (f32[256]{0:T(256)}, f32[256]{0:T(256)S(1)}, u32[]{:S(2)}) copy-start(f32[256]{0:T(256)S(1)} %fusion.95) | copy-start | bytes 3076
  355.8 9.2 copy-start.16
  355.8 9.2 copy-start.20
  379.1 40.3 %collective-permute-start = (bf16[256,3200]{1,0:T(8,128)(2,1)}, bf16[256,3200]{1,0:T(8,128)(2,1)S(1)}, u32[]{:S(2)}, u32[]{:S(2)}) collective-permute-start(bf16[256,3200]{1,0:T(8,128)(2,1)} %get-tuple-element.1295), channel_id=1, source_target_pairs={{0,1},{1,2},{2,3},{3,4},{4,5},{5,6},{6,7},{8,9},{9,10},{10,11},{11... | collective-permute-start | bytes 4915208 | tf_op jit(solution)/shard_map/while/body/eval_jaxpr/ppermute | solution.py:22
  422.0 40.1 %collective-permute-start = (bf16[256,3200]{1,0:T(8,128)(2,1)}, bf16[256,3200]{1,0:T(8,128)(2,1)S(1)}, u32[]{:S(2)}, u32[]{:S(2)}) collective-permute-start(bf16[256,3200]{1,0:T(8,128)(2,1)} %get-tuple-element.1295), channel_id=1, source_target_pairs={{0,1},{1,2},{2,3},{3,4},{4,5},{5,6},{6,7},{8,9},{9,10},{10,11},{11... | collective-permute-start | bytes 4915208 | tf_op jit(solution)/shard_map/while/body/eval_jaxpr/ppermute | solution.py:22
  464.6 39.2 %collective-permute-start = (bf16[256,3200]{1,0:T(8,128)(2,1)}, bf16[256,3200]{1,0:T(8,128)(2,1)S(1)}, u32[]{:S(2)}, u32[]{:S(2)}) collective-permute-start(bf16[256,3200]{1,0:T(8,128)(2,1)} %get-tuple-element.1295), channel_id=1, source_target_pairs={{0,1},{1,2},{2,3},{3,4},{4,5},{5,6},{6,7},{8,9},{9,10},{10,11},{11... | collective-permute-start | bytes 4915208 | tf_op jit(solution)/shard_map/while/body/eval_jaxpr/ppermute | solution.py:22
  506.3 38.4 %collective-permute-start = (bf16[256,3200]{1,0:T(8,128)(2,1)}, bf16[256,3200]{1,0:T(8,128)(2,1)S(1)}, u32[]{:S(2)}, u32[]{:S(2)}) collective-permute-start(bf16[256,3200]{1,0:T(8,128)(2,1)} %get-tuple-element.1295), channel_id=1, source_target_pairs={{0,1},{1,2},{2,3},{3,4},{4,5},{5,6},{6,7},{8,9},{9,10},{10,11},{11... | collective-permute-start | bytes 4915208 | tf_op jit(solution)/shard_map/while/body/eval_jaxpr/ppermute | solution.py:22
  547.3 17.6 slice-start
  635.0 56.1 %copy-start.34 = (f32[1600]{0:T(1024)S(1)}, f32[1600]{0:T(1024)}, u32[]{:S(2)}) copy-start(f32[1600]{0:T(1024)} %get-tuple-element.959) | copy-start | bytes 19204
  695.5 70.6 %copy-start.9 = (f32[256,1600]{0,1:T(8,128)}, f32[256,1600]{0,1:T(8,128)S(1)}, u32[]{:S(2)}) copy-start(f32[256,1600]{0,1:T(8,128)S(1)} %get-tuple-element.1050) | copy-start | bytes 4915204
  695.8 13.8 copy-start.14
  768.1 6.4 copy-start.31
  787.7 8.2 copy-start.4
  787.7 31.2 %copy-start.1 = (bf16[256,25,64]{0,2,1:T(8,128)(2,1)}, bf16[256,25,64]{0,2,1:T(8,128)(2,1)S(1)}, u32[]{:S(2)}) copy-start(bf16[256,25,64]{0,2,1:T(8,128)(2,1)S(1)} %get-tuple-element.1425) | copy-start | bytes 2457604 | tf_op jit(solution)/shard_map/while
  871.1 6.1 copy-start.2
  871.1 6.1 copy-start.5
  877.3 8.2 copy-start.4
  877.3 31.6 %copy-start.1 = (bf16[256,25,64]{0,2,1:T(8,128)(2,1)}, bf16[256,25,64]{0,2,1:T(8,128)(2,1)S(1)}, u32[]{:S(2)}) copy-start(bf16[256,25,64]{0,2,1:T(8,128)(2,1)S(1)} %get-tuple-element.1425) | copy-start | bytes 2457604 | tf_op jit(solution)/shard_map/while
  961.1 6.1 copy-start.2
  961.1 6.1 copy-start.5
  967.3 8.2 copy-start.4
  967.3 31.6 %copy-start.1 = (bf16[256,25,64]{0,2,1:T(8,128)(2,1)}, bf16[256,25,64]{0,2,1:T(8,128)(2,1)S(1)}, u32[]{:S(2)}) copy-start(bf16[256,25,64]{0,2,1:T(8,128)(2,1)S(1)} %get-tuple-element.1425) | copy-start | bytes 2457604 | tf_op jit(solution)/shard_map/while
  1059.9 37.9 %collective-permute-start.1 = (bf16[256,3200]{1,0:T(8,128)(2,1)S(1)}, bf16[256,3200]{1,0:T(8,128)(2,1)S(1)}, u32[]{:S(2)}, u32[]{:S(2)}) collective-permute-start(bf16[256,3200]{1,0:T(8,128)(2,1)S(1)} %fusion.186), channel_id=1, source_target_pairs={{1,0},{2,1},{3,2},{4,3},{5,4},{6,5},{7,6},{9,8},{10,9},{11,10},{12... | collective-permute-start | bytes 4915208 | tf_op jit(solution)/shard_map/while/body/eval_jaxpr/ppermute | solution.py:22
  1103.0 36.7 %collective-permute-start.1 = (bf16[256,3200]{1,0:T(8,128)(2,1)S(1)}, bf16[256,3200]{1,0:T(8,128)(2,1)S(1)}, u32[]{:S(2)}, u32[]{:S(2)}) collective-permute-start(bf16[256,3200]{1,0:T(8,128)(2,1)S(1)} %fusion.186), channel_id=1, source_target_pairs={{1,0},{2,1},{3,2},{4,3},{5,4},{6,5},{7,6},{9,8},{10,9},{11,10},{12... | collective-permute-start | bytes 4915208 | tf_op jit(solution)/shard_map/while/body/eval_jaxpr/ppermute | solution.py:22
  1144.9 35.9 %collective-permute-start.1 = (bf16[256,3200]{1,0:T(8,128)(2,1)S(1)}, bf16[256,3200]{1,0:T(8,128)(2,1)S(1)}, u32[]{:S(2)}, u32[]{:S(2)}) collective-permute-start(bf16[256,3200]{1,0:T(8,128)(2,1)S(1)} %fusion.186), channel_id=1, source_target_pairs={{1,0},{2,1},{3,2},{4,3},{5,4},{6,5},{7,6},{9,8},{10,9},{11,10},{12... | collective-permute-start | bytes 4915208 | tf_op jit(solution)/shard_map/while/body/eval_jaxpr/ppermute | solution.py:22
  1186.0 35.0 %collective-permute-start.1 = (bf16[256,3200]{1,0:T(8,128)(2,1)S(1)}, bf16[256,3200]{1,0:T(8,128)(2,1)S(1)}, u32[]{:S(2)}, u32[]{:S(2)}) collective-permute-start(bf16[256,3200]{1,0:T(8,128)(2,1)S(1)} %fusion.186), channel_id=1, source_target_pairs={{1,0},{2,1},{3,2},{4,3},{5,4},{6,5},{7,6},{9,8},{10,9},{11,10},{12... | collective-permute-start | bytes 4915208 | tf_op jit(solution)/shard_map/while/body/eval_jaxpr/ppermute | solution.py:22
  1240.1 13.3 copy-start.30
  1255.7 6.4 copy-start.26
  1255.7 7.4 copy-start.28
  1471.3 1429.0 %all-to-all-start = ((bf16[32,1,608,1600]{3,2,1,0:T(8,128)(2,1)}), bf16[32,1,608,1600]{3,2,1,0:T(8,128)(2,1)}, u32[]{:S(2)}, u32[]{:S(2)}) async-start(bf16[32,1,608,1600]{3,2,1,0:T(8,128)(2,1)} %bitcast.221), calls=%async_computation | async-start | bytes 129499136 | tf_op jit(solution)/shard_map/all_to_all | solution.py:287
  (26 other events, 102.6 us)
Sparse Core Ops, SparseCore 0:
  10.9 343.4 all-gather.1
where the time goes:
time: 2980 us; the launch traced here: 2930 us
  waiting for transfers between devices  2020 us (68%)
  local copies, waits for them, and re-layouts  445 us (15%)
  matrix products  266 us (9%)
  other arithmetic  144 us (5%)
  starting transfers between devices  38.3 us (1%)
    all_to_all x1, waiting for transfers between devices, per_device(): lax.all_to_all(spread_rows.astype(jnp.bfloat16), ('dp', 'cp'), split_axis...  1400 us
    all_gather x1, waiting for transfers between devices, per_device(): gathered = lax.all_gather(params, ('dp', 'cp'), axis=0, tiled=True)  343 us
    ppermute x8, waiting for transfers between devices, from_behind(): return lax.ppermute(value, axis, pairs)  271 us
    concatenate x2, local copies, waits for them, and re-layouts, per_device(): jnp.concatenate([matmul_tn(grad_qkv, act_one), matmul_tn(grad_attn, mixed...  207 us
    dynamic_slice x9, local copies, waits for them, and re-layouts, pair_rows(): lax.dynamic_slice_in_dim(store, 2 * pair_index, 2, 0)  69.9 us
  transfers between devices with their start and end apart: 10, of which 10 were waited for; matrix products, arithmetic and copies ran while one was open for 1% of the time, Pallas kernels for 0%

commit v1 on v0

--- a/solution.py
+++ b/solution.py
@@ -1,6 +1,10 @@
+import functools
+
 import jax
 import jax.numpy as jnp
 from jax import lax
+from jax.experimental import pallas as pl
+from jax.experimental.pallas import tpu as pltpu
 from jax.sharding import PartitionSpec as P
 
 HEADS = 25
@@ -69,7 +73,7 @@
     return jnp.dot(left_mat, right_mat, preferred_element_type=jnp.float32)
 
 
-def per_device(tokens, params, out_grad, lengths):
+def per_device_general(tokens, params, out_grad, lengths):
     tok_rows, model_width = tokens.shape
     hidden = FF
     head_count = HEADS
@@ -291,9 +295,704 @@
     return (output, input_grad, param_grad)
 
 
+MESH = pl.DeviceIdType.MESH
+GRAIN = 8
+NT = (((1,), (1,)), ((), ()))
+TN = (((0,), (0,)), ((), ()))
+
+
+def dot_nt(a, b):
+    return lax.dot_general(a, b, NT, preferred_element_type=jnp.float32)
+
+
+def dot_tn(a, b):
+    return lax.dot_general(a, b, TN, preferred_element_type=jnp.float32)
+
+
+def dot_nn(a, b):
+    return jnp.dot(a, b, preferred_element_type=jnp.float32)
+
+
+def flat_id(y, c, z, x):
+    return ((y * 2 + c) * 4 + z) * 2 + x
+
+
+def permute(value, move):
+    pairs = []
+    for y in range(2):
+        for c in range(2):
+            for z in range(4):
+                for x in range(2):
+                    to = move(y, c, z, x)
+                    if to is not None:
+                        pairs.append((flat_id(y, c, z, x), flat_id(*to)))
+    return lax.ppermute(value, ("dp", "cp"), pairs)
+
+
+def over_x(value):
+    return permute(value, lambda y, c, z, x: (y, c, z, 1 - x))
+
+
+def over_c(value):
+    return permute(value, lambda y, c, z, x: (y, 1 - c, z, x))
+
+
+def over_cx(value):
+    return permute(value, lambda y, c, z, x: (y, 1 - c, z, 1 - x))
+
+
+def over_y(value):
+    return permute(value, lambda y, c, z, x: (1 - y, c, z, x))
+
+
+def over_z(value, by):
+    return permute(value, lambda y, c, z, x: (y, c, (z + by) % 4, x))
+
+
+class Sizes:
+    def __init__(self, width, hidden, heads, head_size, rows):
+        self.width = width
+        self.hidden = hidden
+        self.heads = heads
+        self.head_size = head_size
+        self.quarter_heads = -(-heads // 4)
+        self.part = self.quarter_heads * head_size
+        self.part_grains = self.part // GRAIN
+        self.width_grains = width // GRAIN
+        self.spill = 4 * self.part_grains - self.width_grains
+        self.qkv = 3 * self.part_grains // 8
+        self.out = self.part_grains // 8
+        self.mlp = hidden // 4 // 8 // GRAIN
+        self.block = rows // GRAIN
+        self.out_start = 3 * self.width_grains
+        self.fc_start = 4 * self.width_grains
+        self.proj_start = self.fc_start + hidden // GRAIN
+        self.vec_start = self.proj_start + hidden // GRAIN
+        self.vec = 2
+        self.used = self.vec_start + self.vec
+
+
+def my_place():
+    dp = lax.axis_index("dp")
+    cp = lax.axis_index("cp")
+    return dp // 2, dp % 2, cp // 2, cp % 2
+
+
+def spread_kernel(sz, p_ref, qkv_ref, out_ref, fc_ref, proj_ref, vec_ref, send_sems, recv_sems):
+    y, c, z, x = my_place()
+    me = flat_id(y, c, z, x)
+
+    def place_of(quarter, share):
+        return (share // 4) * 2 + quarter // 2, (share % 4) * 2 + quarter % 2
+
+    def send(grain, ref, slot, dp, cp, sem, recv):
+        mine = dp * 8 + cp == me
+
+        @pl.when(mine)
+        def _():
+            pltpu.make_async_copy(p_ref.at[grain], ref.at[slot], recv).start()
+
+        @pl.when(jnp.logical_not(mine))
+        def _():
+            copy = pltpu.make_async_remote_copy(
+                src_ref=p_ref.at[grain],
+                dst_ref=ref.at[slot],
+                send_sem=sem,
+                recv_sem=recv,
+                device_id=(dp, cp),
+                device_id_type=MESH,
+            )
+            copy.start()
+
+    def each(grain, act):
+        table = me * sz.block + grain
+
+        def headed(base, parts, ref, recv, share_size):
+            offset = table - base
+            part = offset // sz.width_grains
+            local = offset % sz.width_grains
+
+            def one(quarter, inner, sem):
+                spot = part * sz.part_grains + inner
+                dp, cp = place_of(quarter, spot // share_size)
+                act(grain, ref, spot % share_size, dp, cp, sem, recv)
+
+            @pl.when(jnp.logical_and(offset >= 0, offset < parts * sz.width_grains))
+            def _():
+                one(local // sz.part_grains, local % sz.part_grains, send_sems.at[grain])
+
+                @pl.when(local < sz.spill)
+                def _():
+                    one(3, sz.part_grains - sz.spill + local, send_sems.at[sz.block + grain])
+
+        headed(0, 3, qkv_ref, recv_sems.at[0], sz.qkv)
+        headed(sz.out_start, 1, out_ref, recv_sems.at[1], sz.out)
+
+        def plain(base, ref, recv):
+            offset = table - base
+
+            @pl.when(jnp.logical_and(offset >= 0, offset < 32 * sz.mlp))
+            def _():
+                dp, cp = place_of(offset // (8 * sz.mlp), (offset // sz.mlp) % 8)
+                act(grain, ref, offset % sz.mlp, dp, cp, send_sems.at[grain], recv)
+
+        plain(sz.fc_start, fc_ref, recv_sems.at[2])
+        plain(sz.proj_start, proj_ref, recv_sems.at[3])
+
+    def start(grain, _):
+        each(grain, send)
+        return 0
+
+    lax.fori_loop(0, sz.block, start, 0)
+
+    owner = sz.vec_start // sz.block
+    spot = sz.vec_start % sz.block
+
+    @pl.when(me == owner)
+    def _():
+        def to(device, _):
+            @pl.when(device != me)
+            def _():
+                pltpu.make_async_remote_copy(
+                    src_ref=p_ref.at[pl.ds(spot, sz.vec)],
+                    dst_ref=vec_ref,
+                    send_sem=send_sems.at[2 * sz.block + device],
+                    recv_sem=recv_sems.at[4],
+                    device_id=(device // 8, device % 8),
+                    device_id_type=MESH,
+                ).start()
+
+            return 0
+
+        lax.fori_loop(0, 32, to, 0)
+        pltpu.make_async_copy(p_ref.at[pl.ds(spot, sz.vec)], vec_ref, recv_sems.at[4]).start()
+
+    def sent(grain, ref, slot, dp, cp, sem, recv):
+        @pl.when(dp * 8 + cp != me)
+        def _():
+            pltpu.make_async_copy(p_ref.at[grain], p_ref.at[grain], sem).wait()
+
+    def finish(grain, _):
+        each(grain, sent)
+        return 0
+
+    lax.fori_loop(0, sz.block, finish, 0)
+
+    @pl.when(me == owner)
+    def _():
+        def to(device, _):
+            @pl.when(device != me)
+            def _():
+                pltpu.make_async_copy(vec_ref, vec_ref, send_sems.at[2 * sz.block + device]).wait()
+
+            return 0
+
+        lax.fori_loop(0, 32, to, 0)
+
+    for index, ref in enumerate((qkv_ref, out_ref, fc_ref, proj_ref, vec_ref)):
+        pltpu.make_async_copy(ref, ref, recv_sems.at[index]).wait()
+
+
+def spread(sz, table):
+    width = table.shape[-1]
+    hbm = pl.BlockSpec(memory_space=pl.ANY)
+
+    def like(grains):
+        return jax.ShapeDtypeStruct((grains, GRAIN, width), table.dtype)
+
+    return pl.pallas_call(
+        functools.partial(spread_kernel, sz),
+        out_shape=(like(sz.qkv), like(sz.out), like(sz.mlp), like(sz.mlp), like(sz.vec)),
+        in_specs=[hbm],
+        out_specs=[hbm] * 5,
+        scratch_shapes=[
+            pltpu.SemaphoreType.DMA((2 * sz.block + 32,)),
+            pltpu.SemaphoreType.DMA((5,)),
+        ],
+        compiler_params=pltpu.CompilerParams(has_side_effects=True),
+        name="spread",
+    )(table)
+
+
+def collect_kernel(sz, qkv_ref, out_ref, fc_ref, proj_ref, g_ref, send_sems, recv_sem):
+    y, c, z, x = my_place()
+    me = flat_id(y, c, z, x)
+    quarter = c * 2 + x
+    share = y * 4 + z
+
+    def send(ref, slot, table, sem):
+        dest = table // sz.block
+        mine = dest == me
+
+        @pl.when(mine)
+        def _():
+            pltpu.make_async_copy(ref.at[slot], g_ref.at[table % sz.block], recv_sem).start()
+
+        @pl.when(jnp.logical_not(mine))
+        def _():
+            pltpu.make_async_remote_copy(
+                src_ref=ref.at[slot],
+                dst_ref=g_ref.at[table % sz.block],
+                send_sem=sem,
+                recv_sem=recv_sem,
+                device_id=(dest // 8, dest % 8),
+                device_id_type=MESH,
+            ).start()
+
+    def sent(ref, slot, table, sem):
+        @pl.when(table // sz.block != me)
+        def _():
+            pltpu.make_async_copy(ref.at[slot], ref.at[slot], sem).wait()
+
+    def run(act):
+        def headed(ref, size, base, first_sem):
+            def one(slot, _):
+                spot = share * size + slot
+                part = spot // sz.part_grains
+                local = quarter * sz.part_grains + spot % sz.part_grains
+
+                @pl.when(local < sz.width_grains)
+                def _():
+                    act(ref, slot, base + part * sz.width_grains + local, send_sems.at[first_sem + slot])
+
+                return 0
+
+            lax.fori_loop(0, size, one, 0)
+
+        def plain(ref, base, first_sem):
+            def one(slot, _):
+                table = base + (quarter * 8 + share) * sz.mlp + slot
+                act(ref, slot, table, send_sems.at[first_sem + slot])
+                return 0
+
+            lax.fori_loop(0, sz.mlp, one, 0)
+
+        headed(qkv_ref, sz.qkv, 0, 0)
+        headed(out_ref, sz.out, sz.out_start, sz.qkv)
+        plain(fc_ref, sz.fc_start, sz.qkv + sz.out)
+        plain(proj_ref, sz.proj_start, sz.qkv + sz.out + sz.mlp)
+
+    run(send)
+    run(sent)
+    last = sz.vec_start // sz.block
+
+    @pl.when(me == last)
+    def _():
+        view = g_ref.at[pl.ds(0, sz.vec_start % sz.block)]
+        pltpu.make_async_copy(view, view, recv_sem).wait()
+
+    @pl.when(me != last)
+    def _():
+        pltpu.make_async_copy(g_ref, g_ref, recv_sem).wait()
+
+
+def collect(sz, qkv, out, fc, proj):
+    hbm = pl.BlockSpec(memory_space=pl.ANY)
+    return pl.pallas_call(
+        functools.partial(collect_kernel, sz),
+        out_shape=jax.ShapeDtypeStruct((sz.block, GRAIN, qkv.shape[-1]), qkv.dtype),
+        in_specs=[hbm] * 4,
+        out_specs=hbm,
+        scratch_shapes=[
+            pltpu.SemaphoreType.DMA((sz.qkv + sz.out + 2 * sz.mlp,)),
+            pltpu.SemaphoreType.DMA,
+        ],
+        compiler_params=pltpu.CompilerParams(has_side_effects=True),
+        name="collect",
+    )(qkv, out, fc, proj)
+
+
+def attend_kernel(heads, size, odd_ref, qkv_ref, before_ref, mix_ref, lse_ref):
+    part = heads * size
+    rows = qkv_ref.shape[0]
+    blk = 128
+    scale = size**-0.5
+    lane = lax.broadcasted_iota(jnp.int32, (blk, rows), 1)
+    line = lax.broadcasted_iota(jnp.int32, (blk, rows), 0)
+
+    def block(index, _):
+        first = pl.multiple_of(index * blk, blk)
+        allowed = lane <= line + first
+
+        def one(with_before):
+            for h in range(heads):
+                cols = slice(h * size, (h + 1) * size)
+                keys = slice(part + h * size, part + (h + 1) * size)
+                vals = slice(2 * part + h * size, 2 * part + (h + 1) * size)
+                vals_b = slice(part + h * size, part + (h + 1) * size)
+                q = qkv_ref[pl.ds(first, blk), cols]
+                s = dot_nt(q, qkv_ref[:, keys]) * scale
+                s = jnp.where(allowed, s, MASKED)
+                top = jnp.max(s, axis=-1, keepdims=True)
+                if with_before:
+                    s_b = dot_nt(q, before_ref[:, cols]) * scale
+                    top = jnp.maximum(top, jnp.max(s_b, axis=-1, keepdims=True))
+                    p_b = jnp.exp(s_b - top)
+                p = jnp.exp(s - top)
+                total = jnp.sum(p, axis=-1, keepdims=True)
+                mix = dot_nn(p.astype(jnp.bfloat16), qkv_ref[:, vals])
+                if with_before:
+                    total = total + jnp.sum(p_b, axis=-1, keepdims=True)
+                    mix = mix + dot_nn(p_b.astype(jnp.bfloat16), before_ref[:, vals_b])
+                mix_ref[pl.ds(first, blk), cols] = mix / total
+                lse_ref[pl.ds(first, blk), h : h + 1] = top + jnp.log(total)
+
+        @pl.when(odd_ref[0] == 1)
+        def _():
+            one(True)
+
+        @pl.when(odd_ref[0] == 0)
+        def _():
+            one(False)
+
+        return 0
+
+    lax.fori_loop(0, rows // blk, block, 0)
+
+
+def attend(sz, odd, qkv, before):
+    rows = qkv.shape[0] // 2
+    return pl.pallas_call(
+        functools.partial(attend_kernel, sz.quarter_heads, sz.head_size),
+        grid_spec=pltpu.PrefetchScalarGridSpec(
+            num_scalar_prefetch=1,
+            grid=(2,),
+            in_specs=[
+                pl.BlockSpec((rows, 3 * sz.part), lambda g, odd: (g, 0)),
+                pl.BlockSpec((rows, 2 * sz.part), lambda g, odd: (g, 0)),
+            ],
+            out_specs=[
+                pl.BlockSpec((rows, sz.part), lambda g, odd: (g, 0)),
+                pl.BlockSpec((rows, 8), lambda g, odd: (g, 0)),
+            ],
+        ),
+        out_shape=(
+            jax.ShapeDtypeStruct((2 * rows, sz.part), jnp.float32),
+            jax.ShapeDtypeStruct((2 * rows, 8), jnp.float32),
+        ),
+        cost_estimate=pl.CostEstimate(
+            flops=2 * 2 * 2 * rows * 2 * rows * sz.part,
+            bytes_accessed=20 * rows * sz.part,
+            transcendentals=4 * rows * rows * sz.quarter_heads,
+        ),
+        compiler_params=pltpu.CompilerParams(vmem_limit_bytes=40 << 20),
+        name="attend",
+    )(odd, qkv, before)
+
+
+def attend_back_kernel(heads, size, own, flag_ref, qkv_ref, kv_ref, do_ref, mix_ref, lse_ref, seed_ref, dq_ref, dkv_ref):
+    part = heads * size
+    rows = qkv_ref.shape[0]
+    blk = 128
+    scale = size**-0.5
+    lane = lax.broadcasted_iota(jnp.int32, (blk, rows), 1)
+    line = lax.broadcasted_iota(jnp.int32, (blk, rows), 0)
+    key_start = part if own else 0
+
+    def work():
+        dkv_ref[...] = jnp.zeros_like(dkv_ref)
+
+        def block(index, _):
+            first = pl.multiple_of(index * blk, blk)
+            if own:
+                allowed = lane <= line + first
+            for h in range(heads):
+                cols = slice(h * size, (h + 1) * size)
+                keys = slice(key_start + h * size, key_start + (h + 1) * size)
+                vals = slice(key_start + part + h * size, key_start + part + (h + 1) * size)
+                out_vals = slice(part + h * size, part + (h + 1) * size)
+                q = qkv_ref[pl.ds(first, blk), cols]
+                k = kv_ref[:, keys]
+                do = do_ref[pl.ds(first, blk), cols]
+                s = dot_nt(q, k) * scale
+                p = jnp.exp(s - lse_ref[pl.ds(first, blk), h : h + 1])
+                if own:
+                    p = jnp.where(allowed, p, 0.0)
+                dp = dot_nt(do, kv_ref[:, vals])
+                delta = jnp.sum(
+                    do.astype(jnp.float32) * mix_ref[pl.ds(first, blk), cols], axis=-1, keepdims=True
+                )
+                ds = (p * (dp - delta)).astype(jnp.bfloat16)
+                dq = dot_nn(ds, k) * scale
+                if own:
+                    dq = dq + seed_ref[pl.ds(first, blk), cols]
+                dq_ref[pl.ds(first, blk), cols] = dq.astype(dq_ref.dtype)
+                dkv_ref[:, cols] += dot_tn(ds, q) * scale
+                dkv_ref[:, out_vals] += dot_tn(p.astype(jnp.bfloat16), do)
+            return 0
+
+        lax.fori_loop(0, rows // blk, block, 0)
+
+    if own:
+        work()
+    else:
+
+        @pl.when(flag_ref[0] == 1)
+        def _():
+            work()
+
+        @pl.when(flag_ref[0] == 0)
+        def _():
+            dq_ref[...] = jnp.zeros_like(dq_ref)
+            dkv_ref[...] = jnp.zeros_like(dkv_ref)
+
+
+def attend_back(sz, own, odd, qkv, kv, grad_mix, mix, lse, seed):
+    rows = qkv.shape[0] // 2
+    part = sz.part
+
+    def rows_of(width):
+        return pl.BlockSpec((rows, width), lambda g, odd: (g, 0))
+
+    return pl.pallas_call(
+        functools.partial(attend_back_kernel, sz.quarter_heads, sz.head_size, own),
+        grid_spec=pltpu.PrefetchScalarGridSpec(
+            num_scalar_prefetch=1,
+            grid=(2,),
+            in_specs=[
+                rows_of(3 * part),
+                rows_of(3 * part if own else 2 * part),
+                rows_of(part),
+                rows_of(part),
+                rows_of(8),
+                rows_of(part) if own else pl.BlockSpec((8, 128), lambda g, odd: (0, 0)),
+            ],
+            out_specs=[rows_of(part), rows_of(2 * part)],
+        ),
+        out_shape=(
+            jax.ShapeDtypeStruct((2 * rows, part), jnp.bfloat16 if own else jnp.float32),
+            jax.ShapeDtypeStruct((2 * rows, 2 * part), jnp.float32),
+        ),
+        cost_estimate=pl.CostEstimate(
+            flops=5 * 2 * 2 * rows * rows * part,
+            bytes_accessed=40 * rows * part,
+            transcendentals=2 * rows * rows * sz.quarter_heads,
+        ),
+        compiler_params=pltpu.CompilerParams(vmem_limit_bytes=48 << 20),
+        name="attend_back_own" if own else "attend_back_before",
+    )(odd, qkv, kv, grad_mix, mix, lse, seed)
+
+
+def norm_parts(values):
+    mean = jnp.mean(values, axis=-1, keepdims=True)
+    centre = values - mean
+    rs = lax.rsqrt(jnp.mean(centre * centre, axis=-1, keepdims=True) + EPSILON)
+    return centre * rs, rs
+
+
+def norm_back(normed, rs, grad, gain):
+    e = grad * gain
+    return rs * (
+        e
+        - jnp.mean(e, axis=-1, keepdims=True)
+        - normed * jnp.mean(e * normed, axis=-1, keepdims=True)
+    )
+
+
+def per_device_quad(tokens, params, out_grad, lengths):
+    rows, width = tokens.shape
+    hidden = FF
+    sz = Sizes(width, hidden, HEADS, HEAD_DIM, params.shape[0])
+    y, c, z, x = my_place()
+    quarter = c * 2 + x
+    bf16, f32 = jnp.bfloat16, jnp.float32
+
+    def pick(value, index):
+        return lax.dynamic_index_in_dim(value, index, 0, keepdims=False)
+
+    def put(value, update, index):
+        return lax.dynamic_update_slice_in_dim(value, update[None], index, 0)
+
+    def both(mine, other, index):
+        first = jnp.where(index == 0, mine, other)
+        second = jnp.where(index == 0, other, mine)
+        return jnp.stack([first, second])
+
+    def quad_gather(value):
+        pair = both(value, over_x(value), x)
+        return both(pair, over_c(pair), c)
+
+    def quad_sum(partial):
+        sent = pick(partial, 1 - c).astype(bf16)
+        summed = pick(partial, c) + over_c(sent).astype(f32)
+        sent = pick(summed, 1 - x).astype(bf16)
+        return pick(summed, x) + over_x(sent).astype(f32)
+
+    def quad_exchange(value):
+        got = jnp.zeros_like(value)
+        got = put(got, pick(value, quarter), quarter)
+        got = put(got, over_x(pick(value, quarter ^ 1)), quarter ^ 1)
+        got = put(got, over_c(pick(value, quarter ^ 2)), quarter ^ 2)
+        return put(got, over_cx(pick(value, quarter ^ 3)), quarter ^ 3)
+
+    def gather_relative(share):
+        half = jnp.concatenate([share] + [over_z(share, d) for d in (1, 2, 3)])
+        return jnp.concatenate([half, over_y(half)])
+
+    def gather_ordered(share):
+        half = jnp.zeros((4,) + share.shape, share.dtype)
+        half = put(half, share, z)
+        for d in (1, 2, 3):
+            half = put(half, over_z(share, d), (z - d) % 4)
+        full = both(half, over_y(half), y)
+        return full.reshape((8 * share.shape[0],) + share.shape[1:])
+
+    def reduce_relative(left, right):
+        half = left.shape[1] // 2
+        sent = dot_tn(left[:, half:], right).astype(bf16)
+        kept = dot_tn(left[:, :half], right)
+        summed = kept.reshape(4, half // 4, -1) + over_y(sent).astype(f32).reshape(4, half // 4, -1)
+        total = summed[0]
+        for d in (1, 2, 3):
+            total = total + over_z(summed[d].astype(bf16), -d).astype(f32)
+        return total
+
+    def reduce_ordered(kept, sent):
+        summed = kept + over_y(sent.astype(bf16)).astype(f32)
+        summed = summed.reshape(4, summed.shape[0] // 4, -1)
+        total = pick(summed, z)
+        for d in (1, 2, 3):
+            total = total + over_z(pick(summed, (z + d) % 4).astype(bf16), d).astype(f32)
+        return total
+
+    tok_all = quad_gather(tokens)
+    cot_all = quad_gather(out_grad).reshape(4 * rows, width)
+    s_qkv, s_out, s_fc, s_proj, vec = spread(sz, params.reshape(sz.block, GRAIN, width))
+    flat = lambda value: value.reshape(-1, width)
+    vectors = flat(vec).astype(f32)
+    fc_bias = vectors[8 : 8 + hidden // width].reshape(hidden)
+    w_qkv = gather_ordered(flat(s_qkv))
+    w_out = quad_gather(gather_ordered(flat(s_out))).reshape(-1, width)[:width]
+    w_fc = gather_relative(flat(s_fc))
+    w_proj = gather_relative(flat(s_proj))
+
+    normed_all, _ = norm_parts(tok_all.astype(f32))
+    act_one = (normed_all * vectors[0] + vectors[1]).astype(bf16).reshape(4 * rows, width)
+
+    def quarter_of(vector):
+        padded = jnp.pad(vector, (0, 4 * sz.part - width))
+        return lax.dynamic_slice_in_dim(padded, quarter * sz.part, sz.part, 0)
+
+    qkv_bias = jnp.concatenate(
+        [quarter_of(vectors[2]), jnp.zeros((sz.part,), f32), quarter_of(vectors[3])]
+    )
+    qkv = (dot_nt(act_one, w_qkv) + qkv_bias).astype(bf16)
+    kv = qkv[:, sz.part :]
+    before = permute(kv, lambda py, pc, pz, px: (py, pc, pz + 1, px) if pz % 2 == 0 else None)
+    odd = (z % 2).astype(jnp.int32).reshape(1)
+    mix, lse = attend(sz, odd, qkv, before)
+    mixed = quad_exchange(mix.astype(bf16).reshape(4, rows, sz.part))
+    mixed = jnp.transpose(mixed, (1, 0, 2)).reshape(rows, 4 * sz.part)[:, :width]
+    inputs = tokens.astype(f32)
+    residual = inputs + (dot_nt(mixed, w_out) + vectors[4])
+    normed_two, rs_two = norm_parts(residual)
+    act_two = quad_gather((normed_two * vectors[5] + vectors[6]).astype(bf16)).reshape(4 * rows, width)
+    bias_rel = lax.dynamic_index_in_dim(fc_bias.reshape(4, 2, 4, hidden // 32), quarter, 0, keepdims=False)
+    bias_rel = jnp.where(y == 0, bias_rel, bias_rel[::-1])
+    bias_rel = jnp.stack([lax.dynamic_index_in_dim(bias_rel, (z - d) % 4, 1, keepdims=False) for d in range(4)], 1)
+    pre_act = dot_nt(act_two, w_fc) + bias_rel.reshape(hidden // 4)
+    act_hidden, pull_gelu = jax.vjp(gelu_tanh, pre_act)
+    act_hidden = act_hidden.astype(bf16)
+    g_proj = reduce_relative(act_hidden, cot_all)
+    partial_out = dot_nn(act_hidden, w_proj).reshape(2, 2, rows, width)
+    output = (residual + quad_sum(partial_out) + vectors[7]).astype(bf16)
+
+    cot = out_grad.astype(f32)
+    grad_fc = pull_gelu(dot_nt(cot_all, w_proj))[0].astype(bf16)
+    grad_two = quad_sum(dot_nn(grad_fc, w_fc).reshape(2, 2, rows, width))
+    g_fc = reduce_relative(grad_fc, act_two)
+    grad_res = cot + norm_back(normed_two, rs_two, grad_two, vectors[5])
+    grad_attn = grad_res.astype(bf16)
+    grad_mix = dot_nn(grad_attn, w_out).astype(bf16)
+    grad_mix = jnp.pad(grad_mix, ((0, 0), (0, 4 * sz.part - width)))
+    grad_mix = jnp.transpose(grad_mix.reshape(rows, 4, sz.part), (1, 0, 2))
+    grad_mix = quad_exchange(grad_mix).reshape(4 * rows, sz.part)
+    seed = jnp.zeros((8, 128), f32)
+    dq_before, dkv_before = attend_back(sz, False, odd, qkv, before, grad_mix, mix, lse, seed)
+    returned = permute(
+        dkv_before.astype(bf16), lambda py, pc, pz, px: (py, pc, pz - 1, px) if pz % 2 == 1 else None
+    )
+    dq, dkv = attend_back(sz, True, odd, qkv, qkv, grad_mix, mix, lse, dq_before)
+    grad_qkv = jnp.concatenate([dq, (dkv + returned.astype(f32)).astype(bf16)], axis=1)
+    grad_one = quad_sum(dot_nn(grad_qkv, w_qkv).reshape(2, 2, rows, width))
+
+    half = 3 * sz.part // 2
+    halves = [grad_qkv[:, :half], grad_qkv[:, half:]]
+    mine = jnp.where(y == 0, halves[0], halves[1])
+    other = jnp.where(y == 0, halves[1], halves[0])
+    g_qkv = reduce_ordered(dot_tn(mine, act_one), dot_tn(other, act_one))
+
+    g_out = jnp.pad(dot_tn(grad_attn, mixed), ((0, 4 * sz.part - width), (0, 0))).reshape(2, 2, sz.part, width)
+    g_out = quad_sum(g_out).reshape(2, sz.part // 2, width)
+    g_out = reduce_ordered(pick(g_out, y), pick(g_out, 1 - y))
+
+    normed_one, rs_one = norm_parts(inputs)
+    input_grad = (grad_res + norm_back(normed_one, rs_one, grad_one, vectors[0])).astype(bf16)
+
+    def placed(vector):
+        spot = lax.dynamic_update_slice_in_dim(jnp.zeros((4 * sz.part,), f32), vector, quarter * sz.part, 0)
+        return spot[:width]
+
+    sums = jnp.sum(grad_qkv.astype(f32), axis=0)
+    bias_sum = jnp.sum(grad_fc.astype(f32), axis=0).reshape(2, 4, hidden // 32)
+    ordered = jnp.stack([lax.dynamic_index_in_dim(bias_sum, (z - k) % 4, 1, keepdims=False) for k in range(4)], 1)
+    ordered = jnp.where(y == 0, ordered, ordered[::-1]).reshape(1, hidden // 4)
+    fc_rows = lax.dynamic_update_slice_in_dim(jnp.zeros((4, hidden // 4), f32), ordered, quarter, 0)
+    grad_vectors = jnp.concatenate(
+        [
+            jnp.stack(
+                [
+                    jnp.sum(grad_one * normed_one, axis=0),
+                    jnp.sum(grad_one, axis=0),
+                    placed(sums[: sz.part]),
+                    placed(sums[2 * sz.part :]),
+                    jnp.sum(grad_attn.astype(f32), axis=0),
+                    jnp.sum(grad_two * normed_two, axis=0),
+                    jnp.sum(grad_two, axis=0),
+                    jnp.sum(cot, axis=0),
+                ]
+            ),
+            fc_rows.reshape(hidden // width, width),
+        ]
+    )
+    grad_vectors = lax.psum(grad_vectors, ("dp", "cp"))
+
+    grains = lambda value: value.astype(bf16).reshape(-1, GRAIN, width)
+    table = collect(sz, grains(g_qkv), grains(g_out), grains(g_fc), grains(g_proj))
+    table = table.reshape(sz.block * GRAIN, width).astype(f32)
+    used = (sz.vec_start % sz.block) * GRAIN
+    tail = jnp.concatenate(
+        [grad_vectors, jnp.zeros((sz.block * GRAIN - used - grad_vectors.shape[0], width), f32)]
+    )
+    last = flat_id(y, c, z, x) == sz.vec_start // sz.block
+    tail = jnp.where(last, tail, table[used:])
+    param_grad = jnp.concatenate([table[:used], tail])
+    return (output, input_grad, param_grad)
+
+
+def fits_quad(mesh, tokens, params, lengths):
+    dp, cp = mesh.shape["dp"], mesh.shape["cp"]
+    rows = tokens.shape[0] // (dp * cp)
+    width = tokens.shape[1]
+    blocks = params.shape[0] // (dp * cp)
+    return (
+        (dp, cp) == (4, 8)
+        and lengths.shape[1] == 2
+        and rows * cp == lengths.shape[1] * MIN_LEN
+        and rows % 128 == 0
+        and blocks % GRAIN == 0
+        and (HEADS, HEAD_DIM, FF, width) == (25, 64, 6400, 1600)
+    )
+
+
 def solution(mesh):
     in_specs = (P(("dp", "cp"), None), P(("dp", "cp"), None), P(("dp", "cp"), None), P("dp", None))
     out_specs = (P(("dp", "cp"), None), P(("dp", "cp"), None), P(("dp", "cp"), None))
-    return jax.shard_map(
-        per_device, mesh=mesh, in_specs=in_specs, out_specs=out_specs, check_vma=False
-    )
+
+    def step(tokens, params, out_grad, lengths):
+        body = per_device_quad if fits_quad(mesh, tokens, params, lengths) else per_device_general
+        return jax.shard_map(
+            body, mesh=mesh, in_specs=in_specs, out_specs=out_specs, check_vma=False
+        )(tokens, params, out_grad, lengths)
+
+    return step

time: 2980 us -> 1020 us (0.34); the launches traced: 2930 us -> 1020 us
  waiting for transfers between devices: 2020 us -> 349 us
  local copies, waits for them, and re-layouts: 445 us -> 124 us
  Pallas kernels: 0 us -> 180 us
  matrix products: 266 us -> 89.9 us
  starting transfers between devices: 38.3 us -> 153 us
  other arithmetic: 144 us -> 104 us
    all_to_all x1 -> x0, waiting for transfers between devices: 1400 us -> none  [per_device(): lax.all_to_all(spread_rows.astype(jnp.bfloat16), ('dp', 'cp'), split_axis...]
    all_gather x1 -> x0, waiting for transfers between devices: 343 us -> none  [per_device(): gathered = lax.all_gather(params, ('dp', 'cp'), axis=0, tiled=True)]
    concatenate x9 -> x4, local copies, waits for them, and re-layouts: 234 us -> 9.07 us  [the longest x2 7.05 us: gather_relative(): return jnp.concatenate([half, over_y(half)])]
    dot_general x33 -> x14, matrix products: 266 us -> 84.2 us  [the longest x6 30.3 us: dot_tn(): return lax.dot_general(a, b, TN, preferred_element_type=jnp.float32)]
    pallas_call x0 -> x5, Pallas kernels: none -> 180 us  [the longest x2 66.5 us: attend_back(): pl.pallas_call(functools.partial(attend_back_kernel, sz.quarter_heads, sz...]
    ppermute x8 -> x56, starting transfers between devices: 32.3 us -> 153 us  [permute(): return lax.ppermute(value, ('dp', 'cp'), pairs)]
    psum x0 -> x1, waiting for transfers between devices: none -> 64.6 us  [per_device_quad(): grad_vectors = lax.psum(grad_vectors, ('dp', 'cp'))]
    dynamic_slice x9 -> x13, local copies, waits for them, and re-layouts: 69.9 us -> 20.5 us  [the longest x10 19.7 us: pick(): return lax.dynamic_index_in_dim(value, index, 0, keepdims=False)]
  transfers between devices with their start and end apart: 10 -> 57, of which waited for: 10 -> 21; matrix products, arithmetic and copies ran while one was open for 1% -> 24% of each run, Pallas kernels for 0% -> 13%
where the time goes in v1:
time: 1020 us
  waiting for transfers between devices  349 us (34%)
  Pallas kernels  180 us (18%)
  starting transfers between devices  153 us (15%)
  local copies, waits for them, and re-layouts  124 us (12%)
  other arithmetic  104 us (10%)
  matrix products  89.9 us (9%)
  between operations  15.8 us (2%)
    ppermute x56, waiting for transfers between devices, permute(): return lax.ppermute(value, ('dp', 'cp'), pairs)  285 us
    ppermute x56, starting transfers between devices, permute(): return lax.ppermute(value, ('dp', 'cp'), pairs)  153 us
    pallas_call x2, Pallas kernels, attend_back(): pl.pallas_call(functools.partial(attend_back_kernel, sz.quarter_heads, sz...  66.5 us
    psum x1, waiting for transfers between devices, per_device_quad(): grad_vectors = lax.psum(grad_vectors, ('dp', 'cp'))  64.6 us
    pallas_call x1, Pallas kernels, spread(): pl.pallas_call(functools.partial(spread_kernel, sz), out_shape=(like(sz.q...  45.8 us
    pallas_call x1, Pallas kernels, collect(): pl.pallas_call(functools.partial(collect_kernel, sz), out_shape=jax.Shape...  44.1 us
    dot_general x6, matrix products, dot_tn(): return lax.dot_general(a, b, TN, preferred_element_type=jnp.float32)  30.3 us
    dot_general x4, matrix products, dot_nt(): return lax.dot_general(a, b, NT, preferred_element_type=jnp.float32)  30.3 us
  transfers between devices with their start and end apart: 57, of which 21 were waited for; matrix products, arithmetic and copies ran while one was open for 24% of the time, Pallas kernels for 13%

profile of v1, /device:TPU:10, one launch (start us, length us, event | category | flops | bytes accessed | tf_op | source)
XLA Modules:
  0.0 1016.1 jit_solution(2610644040538324857)
XLA Ops:
  7.2 45.8 %spread.1 = (bf16[21,8,1600]{2,1,0:T(8,128)(2,1)}, bf16[7,8,1600]{2,1,0:T(8,128)(2,1)}, bf16[25,8,1600]{2,1,0:T(8,128)(2,1)}, bf16[25,8,1600]{2,1,0:T(8,128)(2,1)}, bf16[2,8,1600]{2,1,0:T(8,128)(2,1)}) custom-call(bf16[76,8,1600]{2,1,0:T(8,128)(2,1)} %bitcast.344), custom_call_target="tpu_custom_call" | custom-call | tf_op jit(solution)/shard_map/spread/pallas_call | solution.py:503
  79.1 9.2 collective-permute-start
  89.2 14.1 %collective-permute-done.12 = bf16[56,1600]{1,0:T(8,128)(2,1)} collective-permute-done((bf16[56,1600]{1,0:T(8,128)(2,1)}, bf16[56,1600]{1,0:T(8,128)(2,1)}, u32[]{:S(2)}, u32[]{:S(2)}) %collective-permute-start.12) | collective-permute-done | bytes 179232 | tf_op jit(solution)/shard_map/ppermute | solution.py:329
  114.5 8.0 collective-permute-done.3
  126.8 19.2 %collective-permute-start.20 = (bf16[200,1600]{1,0:T(8,128)(2,1)}, bf16[200,1600]{1,0:T(8,128)(2,1)S(1)}, u32[]{:S(2)}, u32[]{:S(2)}) collective-permute-start(bf16[200,1600]{1,0:T(8,128)(2,1)} %bitcast.342), channel_id=1, source_target_pairs={{0,6},{1,7},{2,0},{3,1},{4,2},{5,3},{6,4},{7,5},{8,14},{9,15},{10,... | collective-permute-start | bytes 1920008 | tf_op jit(solution)/shard_map/ppermute | solution.py:329
  157.0 22.7 %collective-permute-done.19 = bf16[200,1600]{1,0:T(8,128)(2,1)S(1)} collective-permute-done((bf16[200,1600]{1,0:T(8,128)(2,1)}, bf16[200,1600]{1,0:T(8,128)(2,1)S(1)}, u32[]{:S(2)}, u32[]{:S(2)}) %collective-permute-start.19) | collective-permute-done | bytes 640032 | tf_op jit(solution)/shard_map/ppermute | solution.py:329
  179.7 37.7 %collective-permute-start.13 = (bf16[4,56,1600]{2,1,0:T(8,128)(2,1)S(1)}, bf16[4,56,1600]{2,1,0:T(8,128)(2,1)S(1)}, u32[]{:S(2)}, u32[]{:S(2)}) collective-permute-start(bf16[4,56,1600]{2,1,0:T(8,128)(2,1)S(1)} %bitcast_dynamic-update-slice_fusion.11), channel_id=1, source_target_pairs={{0,16},{1,17},{2,18},{3,19},{4,20},{5,21},{6,22},{7,23},{8,24},{9,... | collective-permute-start | bytes 2150408 | tf_op jit(solution)/shard_map/ppermute | solution.py:329
  223.6 8.1 collective-permute-start.5
  259.7 21.7 %collective-permute-done.5 = bf16[4,168,1600]{2,1,0:T(8,128)(2,1)} collective-permute-done((bf16[4,168,1600]{2,1,0:T(8,128)(2,1)}, bf16[4,168,1600]{2,1,0:T(8,128)(2,1)}, u32[]{:S(2)}, u32[]{:S(2)}) %collective-permute-start.5) | collective-permute-done | bytes 2150432 | tf_op jit(solution)/shard_map/ppermute | solution.py:329
  305.8 25.8 %collective-permute-done.6.before_ref.kv_ref = bf16[1024,896]{1,0:T(8,128)(2,1)S(1)} collective-permute-done((bf16[1024,896]{1,0:T(8,128)(2,1)S(1)}, bf16[1024,896]{1,0:T(8,128)(2,1)S(1)}, u32[]{:S(2)}, u32[]{:S(2)}) %collective-permute-start.6) | collective-permute-done | bytes 1835040 | tf_op jit(solution)/shard_map/ppermute | solution.py:329
  331.6 23.3 %attend.1 = (f32[1024,448]{1,0:T(8,128)S(1)}, f32[1024,8]{1,0:T(8,128)S(1)}) custom-call(s32[1]{0:T(128)} %bitcast.odd_ref.flag_ref, bf16[1024,1344]{1,0:T(8,128)(2,1)S(1)} %add_convert_fusion.1.qkv_ref.kv_ref, bf16[1024,896]{1,0:T(8,128)(2,1)S(1)} %collective-permute-done.6.before_ref.kv_ref), custom_call_target="tpu_custom_call" | custom-call | flops 1879048192 | bytes 4587520 | tf_op jit(solution)/shard_map/attend/pallas_call | solution.py:655
  394.0 10.1 collective-permute-done.16
  411.8 7.4 copy.30
  440.4 9.3 fusion.97
  449.6 13.3 %convert_reduce_fusion = (f32[1600]{0:T(1024)S(1)}, bf16[1024,1600]{0,1:T(8,128)(2,1)S(1)}, bf16[1024,1600]{0,1:T(8,128)(2,1)S(1)}) fusion(f32[1024,1600]{0,1:T(8,128)S(1)} %fusion.97, f32[1600]{0:T(1024)S(1)} %copy-done.76, bf16[1024,1600]{1,0:T(8,128)(2,1)S(1)} %bitcast.327, bf16[1600,1600]{1,0:T(8,128)(2,1)} %constant_dynamic-update-slice_fusion.5), kind=kOutput, calls=%fused_computation.15 | convolution fusion | flops 5290392064 | bytes 21516800 | tf_op jit(solution)/shard_map/dot_general | solution.py:305
  479.4 6.9 fusion.99
  512.4 6.9 fusion.102
  533.9 14.9 %collective-permute-done.31 = bf16[256,1600]{0,1:T(8,128)(2,1)} collective-permute-done((bf16[256,1600]{0,1:T(8,128)(2,1)}, bf16[256,1600]{0,1:T(8,128)(2,1)}, u32[]{:S(2)}, u32[]{:S(2)}) %collective-permute-start.31) | collective-permute-done | bytes 819232 | tf_op jit(solution)/shard_map/ppermute | solution.py:329
  551.7 14.0 %collective-permute-done.27 = bf16[256,1600]{0,1:T(8,128)(2,1)S(1)} collective-permute-done((bf16[256,1600]{0,1:T(8,128)(2,1)}, bf16[256,1600]{0,1:T(8,128)(2,1)S(1)}, u32[]{:S(2)}, u32[]{:S(2)}) %collective-permute-start.27) | collective-permute-done | bytes 819232 | tf_op jit(solution)/shard_map/ppermute | solution.py:329
  577.8 9.3 pad.19.clone
  599.5 16.3 %collective-permute-done.48 = bf16[800,1600]{1,0:T(8,128)(2,1)} collective-permute-done((bf16[800,1600]{1,0:T(8,128)(2,1)}, bf16[800,1600]{1,0:T(8,128)(2,1)}, u32[]{:S(2)}, u32[]{:S(2)}) %collective-permute-start.48) | collective-permute-done | bytes 2560032 | tf_op jit(solution)/shard_map/ppermute | solution.py:329
  628.4 32.3 %attend_back_before.1 = (f32[1024,448]{1,0:T(8,128)S(1)}, f32[1024,896]{1,0:T(8,128)}) custom-call(s32[1]{0:T(128)} %bitcast.odd_ref.flag_ref, bf16[1024,1344]{1,0:T(8,128)(2,1)} %copy-done, bf16[1024,896]{1,0:T(8,128)(2,1)S(1)} %copy-done.5, bf16[1024,448]{1,0:T(8,128)(2,1)S(1)} %bitcast.297, f32[1024,448]{1,0:T(8,128)} %copy-done.1, ...), custom_call_target="tpu_custom_call" | custom-call | flops 2348810240 | bytes 9175040 | tf_op jit(solution)/shard_map/attend_back_before/pallas_call | solution.py:747
  668.6 34.1 %attend_back_own.1 = (bf16[1024,448]{1,0:T(8,128)(2,1)S(1)}, f32[1024,896]{1,0:T(8,128)}) custom-call(s32[1]{0:T(128)} %bitcast.odd_ref.flag_ref, bf16[1024,1344]{1,0:T(8,128)(2,1)} %copy-done, bf16[1024,1344]{1,0:T(8,128)(2,1)} %copy-done, bf16[1024,448]{1,0:T(8,128)(2,1)S(1)} %bitcast.298, f32[1024,448]{1,0:T(8,128)S(1)} %copy-done.2, ...), custom_call_target="tpu_custom_call" | custom-call | flops 2348810240 | bytes 9175040 | tf_op jit(solution)/shard_map/attend_back_own/pallas_call | solution.py:747
  705.9 28.0 %collective-permute-done.49 = bf16[200,1600]{1,0:T(8,128)(2,1)S(1)} collective-permute-done((bf16[200,1600]{1,0:T(8,128)(2,1)S(1)}, bf16[200,1600]{1,0:T(8,128)(2,1)S(1)}, u32[]{:S(2)}, u32[]{:S(2)}) %collective-permute-start.49) | collective-permute-done | bytes 640032 | tf_op jit(solution)/shard_map/ppermute | solution.py:329
  738.8 7.6 fusion.100
  762.5 41.8 %collective-permute-done.38 = bf16[672,1600]{1,0:T(8,128)(2,1)} collective-permute-done((bf16[672,1600]{1,0:T(8,128)(2,1)}, bf16[672,1600]{1,0:T(8,128)(2,1)}, u32[]{:S(2)}, u32[]{:S(2)}) %collective-permute-start.38) | collective-permute-done | bytes 2150432 | tf_op jit(solution)/shard_map/ppermute | solution.py:329
  810.4 17.3 %collective-permute-start.40 = (bf16[168,1600]{1,0:T(8,128)(2,1)}, bf16[168,1600]{1,0:T(8,128)(2,1)}, u32[]{:S(2)}, u32[]{:S(2)}) collective-permute-start(bf16[168,1600]{1,0:T(8,128)(2,1)} %get-tuple-element.56), channel_id=1, source_target_pairs={{0,4},{1,5},{2,6},{3,7},{4,0},{5,1},{6,2},{7,3},{8,12},{9,13},{10,... | collective-permute-start | bytes 1612808 | tf_op jit(solution)/shard_map/ppermute | solution.py:329
  835.1 11.3 %collective-permute-done.44 = bf16[224,1600]{1,0:T(8,128)(2,1)} collective-permute-done((bf16[224,1600]{1,0:T(8,128)(2,1)S(1)}, bf16[224,1600]{1,0:T(8,128)(2,1)}, u32[]{:S(2)}, u32[]{:S(2)}) %collective-permute-start.44) | collective-permute-done | bytes 716832 | tf_op jit(solution)/shard_map/ppermute | solution.py:329
  851.6 14.3 %collective-permute-done.40 = bf16[168,1600]{1,0:T(8,128)(2,1)} collective-permute-done((bf16[168,1600]{1,0:T(8,128)(2,1)}, bf16[168,1600]{1,0:T(8,128)(2,1)}, u32[]{:S(2)}, u32[]{:S(2)}) %collective-permute-start.40) | collective-permute-done | bytes 537632 | tf_op jit(solution)/shard_map/ppermute | solution.py:329
  865.9 19.0 %collective-permute-done.41 = bf16[168,1600]{1,0:T(8,128)(2,1)} collective-permute-done((bf16[168,1600]{1,0:T(8,128)(2,1)}, bf16[168,1600]{1,0:T(8,128)(2,1)}, u32[]{:S(2)}, u32[]{:S(2)}) %collective-permute-start.41) | collective-permute-done | bytes 537632 | tf_op jit(solution)/shard_map/ppermute | solution.py:329
  892.6 44.1 %collect.1 = bf16[76,8,1600]{2,1,0:T(8,128)(2,1)} custom-call(bf16[21,8,1600]{2,1,0:T(8,128)(2,1)} %fusion.77.qkv_ref, bf16[7,8,1600]{2,1,0:T(8,128)(2,1)} %fusion.84.out_ref, bf16[25,8,1600]{2,1,0:T(8,128)(2,1)} %fusion.72.fc_ref, bf16[25,8,1600]{2,1,0:T(8,128)(2,1)} %fusion.73.proj_ref), custom_call_target="tpu_custom_call" | custom-call | tf_op jit(solution)/shard_map/collect/pallas_call | solution.py:591
  940.7 64.6 %all-reduce.7.cloned.1.call-done = f32[12,1600]{1,0:T(8,128)} async-done(((f32[12,1600]{1,0:T(8,128)}), f32[12,1600]{1,0:T(8,128)}) %all-reduce.7.cloned.1.call-update) | async-done | bytes 76816 | tf_op jit(solution)/shard_map/psum | solution.py:958
  (460 shorter events, 342.0 us)
Async XLA Ops:
  7.2 998.1 %all-reduce.7.cloned.1.call-start = ((), (), s32[]{:S(2)}) async-start(), calls=%async_computation | async-start | bytes 212992 | tf_op jit(solution)/shard_map/psum | solution.py:958
  63.6 58.9 %collective-permute-start.3 = (bf16[168,1600]{1,0:T(8,128)(2,1)}, bf16[168,1600]{1,0:T(8,128)(2,1)S(1)}, u32[]{:S(2)}, u32[]{:S(2)}) collective-permute-start(bf16[168,1600]{1,0:T(8,128)(2,1)} %bitcast.352), channel_id=1, source_target_pairs={{0,4},{1,5},{2,6},{3,7},{4,0},{5,1},{6,2},{7,3},{8,12},{9,13},{10,... | collective-permute-start | bytes 1612808 | tf_op jit(solution)/shard_map/ppermute | solution.py:329
  78.1 77.5 %collective-permute-start.4 = (bf16[168,1600]{1,0:T(8,128)(2,1)S(1)}, bf16[168,1600]{1,0:T(8,128)(2,1)S(1)}, u32[]{:S(2)}, u32[]{:S(2)}) collective-permute-start(bf16[168,1600]{1,0:T(8,128)(2,1)S(1)} %bitcast.353), channel_id=1, source_target_pairs={{0,6},{1,7},{2,0},{3,1},{4,2},{5,3},{6,4},{7,5},{8,14},{9,15},{10,... | collective-permute-start | bytes 1612808 | tf_op jit(solution)/shard_map/ppermute | solution.py:329
  106.8 48.8 %collective-permute-start.18 = (bf16[200,1600]{1,0:T(8,128)(2,1)}, bf16[200,1600]{1,0:T(8,128)(2,1)S(1)}, u32[]{:S(2)}, u32[]{:S(2)}) collective-permute-start(bf16[200,1600]{1,0:T(8,128)(2,1)} %bitcast.340), channel_id=1, source_target_pairs={{0,2},{1,3},{2,4},{3,5},{4,6},{5,7},{6,0},{7,1},{8,10},{9,11},{10,... | collective-permute-start | bytes 1920008 | tf_op jit(solution)/shard_map/ppermute | solution.py:329
  122.6 57.1 %collective-permute-start.19 = (bf16[200,1600]{1,0:T(8,128)(2,1)}, bf16[200,1600]{1,0:T(8,128)(2,1)S(1)}, u32[]{:S(2)}, u32[]{:S(2)}) collective-permute-start(bf16[200,1600]{1,0:T(8,128)(2,1)} %bitcast.341), channel_id=1, source_target_pairs={{0,4},{1,5},{2,6},{3,7},{4,0},{5,1},{6,2},{7,3},{8,12},{9,13},{10,... | collective-permute-start | bytes 1920008 | tf_op jit(solution)/shard_map/ppermute | solution.py:329
  126.8 90.6 %collective-permute-start.20 = (bf16[200,1600]{1,0:T(8,128)(2,1)}, bf16[200,1600]{1,0:T(8,128)(2,1)S(1)}, u32[]{:S(2)}, u32[]{:S(2)}) collective-permute-start(bf16[200,1600]{1,0:T(8,128)(2,1)} %bitcast.342), channel_id=1, source_target_pairs={{0,6},{1,7},{2,0},{3,1},{4,2},{5,3},{6,4},{7,5},{8,14},{9,15},{10,... | collective-permute-start | bytes 1920008 | tf_op jit(solution)/shard_map/ppermute | solution.py:329
  146.0 77.5 %collective-permute-start.22 = (bf16[200,1600]{1,0:T(8,128)(2,1)}, bf16[200,1600]{1,0:T(8,128)(2,1)S(1)}, u32[]{:S(2)}, u32[]{:S(2)}) collective-permute-start(bf16[200,1600]{1,0:T(8,128)(2,1)} %bitcast.336), channel_id=1, source_target_pairs={{0,2},{1,3},{2,4},{3,5},{4,6},{5,7},{6,0},{7,1},{8,10},{9,11},{10,... | collective-permute-start | bytes 1920008 | tf_op jit(solution)/shard_map/ppermute | solution.py:329
  155.7 81.0 %collective-permute-start.23 = (bf16[200,1600]{1,0:T(8,128)(2,1)S(1)}, bf16[200,1600]{1,0:T(8,128)(2,1)S(1)}, u32[]{:S(2)}, u32[]{:S(2)}) collective-permute-start(bf16[200,1600]{1,0:T(8,128)(2,1)S(1)} %bitcast.337), channel_id=1, source_target_pairs={{0,4},{1,5},{2,6},{3,7},{4,0},{5,1},{6,2},{7,3},{8,12},{9,13},{10,... | collective-permute-start | bytes 1920008 | tf_op jit(solution)/shard_map/ppermute | solution.py:329
  155.7 87.5 %collective-permute-start.24 = (bf16[200,1600]{1,0:T(8,128)(2,1)S(1)}, bf16[200,1600]{1,0:T(8,128)(2,1)S(1)}, u32[]{:S(2)}, u32[]{:S(2)}) collective-permute-start(bf16[200,1600]{1,0:T(8,128)(2,1)S(1)} %bitcast.338), channel_id=1, source_target_pairs={{0,6},{1,7},{2,0},{3,1},{4,2},{5,3},{6,4},{7,5},{8,14},{9,15},{10,... | collective-permute-start | bytes 1920008 | tf_op jit(solution)/shard_map/ppermute | solution.py:329
  179.7 68.8 %collective-permute-start.13 = (bf16[4,56,1600]{2,1,0:T(8,128)(2,1)S(1)}, bf16[4,56,1600]{2,1,0:T(8,128)(2,1)S(1)}, u32[]{:S(2)}, u32[]{:S(2)}) collective-permute-start(bf16[4,56,1600]{2,1,0:T(8,128)(2,1)S(1)} %bitcast_dynamic-update-slice_fusion.11), channel_id=1, source_target_pairs={{0,16},{1,17},{2,18},{3,19},{4,20},{5,21},{6,22},{7,23},{8,24},{9,... | collective-permute-start | bytes 2150408 | tf_op jit(solution)/shard_map/ppermute | solution.py:329
  223.6 57.9 %collective-permute-start.5 = (bf16[4,168,1600]{2,1,0:T(8,128)(2,1)}, bf16[4,168,1600]{2,1,0:T(8,128)(2,1)}, u32[]{:S(2)}, u32[]{:S(2)}) collective-permute-start(bf16[4,168,1600]{2,1,0:T(8,128)(2,1)} %bitcast_dynamic-update-slice_fusion), channel_id=1, source_target_pairs={{0,16},{1,17},{2,18},{3,19},{4,20},{5,21},{6,22},{7,23},{8,24},{9,... | collective-permute-start | bytes 6451208 | tf_op jit(solution)/shard_map/ppermute | solution.py:329
  236.6 187.6 %collective-permute-start.21 = (bf16[800,1600]{1,0:T(8,128)(2,1)}, bf16[800,1600]{1,0:T(8,128)(2,1)}, u32[]{:S(2)}, u32[]{:S(2)}) collective-permute-start(bf16[800,1600]{1,0:T(8,128)(2,1)} %pad_maximum_fusion.8), channel_id=1, source_target_pairs={{0,16},{1,17},{2,18},{3,19},{4,20},{5,21},{6,22},{7,23},{8,24},{9,... | collective-permute-start | bytes 7680008 | tf_op jit(solution)/shard_map/ppermute | solution.py:329
  248.5 179.2 %collective-permute-start.25 = (bf16[800,1600]{1,0:T(8,128)(2,1)}, bf16[800,1600]{1,0:T(8,128)(2,1)}, u32[]{:S(2)}, u32[]{:S(2)}) collective-permute-start(bf16[800,1600]{1,0:T(8,128)(2,1)} %pad_maximum_fusion.9), channel_id=1, source_target_pairs={{0,16},{1,17},{2,18},{3,19},{4,20},{5,21},{6,22},{7,23},{8,24},{9,... | collective-permute-start | bytes 7680008 | tf_op jit(solution)/shard_map/ppermute | solution.py:329
  300.3 75.2 %collective-permute-start.15 = (bf16[2,448,1600]{2,1,0:T(8,128)(2,1)}, bf16[2,448,1600]{2,1,0:T(8,128)(2,1)}, u32[]{:S(2)}, u32[]{:S(2)}) collective-permute-start(bf16[2,448,1600]{2,1,0:T(8,128)(2,1)} %pad_maximum_fusion.7), channel_id=1, source_target_pairs={{0,8},{1,9},{2,10},{3,11},{4,12},{5,13},{6,14},{7,15},{8,0},{9,1},... | collective-permute-start | bytes 8601608 | tf_op jit(solution)/shard_map/ppermute | solution.py:329
  498.3 95.0 %collective-permute-start.52 = (bf16[800,1600]{1,0:T(8,128)(2,1)}, bf16[800,1600]{1,0:T(8,128)(2,1)}, u32[]{:S(2)}, u32[]{:S(2)}) collective-permute-start(bf16[800,1600]{1,0:T(8,128)(2,1)} %convolution_convert_fusion), channel_id=1, source_target_pairs={{0,16},{1,17},{2,18},{3,19},{4,20},{5,21},{6,22},{7,23},{8,24},{9,... | collective-permute-start | bytes 7680008 | tf_op jit(solution)/shard_map/ppermute | solution.py:329
  498.3 117.5 %collective-permute-start.48 = (bf16[800,1600]{1,0:T(8,128)(2,1)}, bf16[800,1600]{1,0:T(8,128)(2,1)}, u32[]{:S(2)}, u32[]{:S(2)}) collective-permute-start(bf16[800,1600]{1,0:T(8,128)(2,1)} %convolution_convert_fusion.1), channel_id=1, source_target_pairs={{0,16},{1,17},{2,18},{3,19},{4,20},{5,21},{6,22},{7,23},{8,24},{9,... | collective-permute-start | bytes 7680008 | tf_op jit(solution)/shard_map/ppermute | solution.py:329
  569.8 54.8 %collective-permute-start.32 = (bf16[256,448]{0,1:T(8,128)(2,1)S(1)}, bf16[256,448]{0,1:T(8,128)(2,1)S(1)}, u32[]{:S(2)}, u32[]{:S(2)}) collective-permute-start(bf16[256,448]{0,1:T(8,128)(2,1)S(1)} %get-tuple-element.91), channel_id=1, source_target_pairs={{0,1},{1,0},{2,3},{3,2},{4,5},{5,4},{6,7},{7,6},{8,9},{9,8},{10,11... | collective-permute-start | bytes 688136 | tf_op jit(solution)/shard_map/ppermute | solution.py:329
  571.7 53.7 %collective-permute-start.33 = (bf16[256,448]{0,1:T(8,128)(2,1)S(1)}, bf16[256,448]{0,1:T(8,128)(2,1)S(1)}, u32[]{:S(2)}, u32[]{:S(2)}) collective-permute-start(bf16[256,448]{0,1:T(8,128)(2,1)S(1)} %get-tuple-element.90), channel_id=1, source_target_pairs={{0,8},{1,9},{2,10},{3,11},{4,12},{5,13},{6,14},{7,15},{8,0},{9,1},... | collective-permute-start | bytes 688136 | tf_op jit(solution)/shard_map/ppermute | solution.py:329
  571.7 54.4 %collective-permute-start.34 = (bf16[256,448]{0,1:T(8,128)(2,1)S(1)}, bf16[256,448]{0,1:T(8,128)(2,1)S(1)}, u32[]{:S(2)}, u32[]{:S(2)}) collective-permute-start(bf16[256,448]{0,1:T(8,128)(2,1)S(1)} %get-tuple-element.89), channel_id=1, source_target_pairs={{0,9},{1,8},{2,11},{3,10},{4,13},{5,12},{6,15},{7,14},{8,1},{9,0},... | collective-permute-start | bytes 688136 | tf_op jit(solution)/shard_map/ppermute | solution.py:329
  599.5 66.1 %collective-permute-start.53 = (bf16[200,1600]{1,0:T(8,128)(2,1)}, bf16[200,1600]{1,0:T(8,128)(2,1)}, u32[]{:S(2)}, u32[]{:S(2)}) collective-permute-start(bf16[200,1600]{1,0:T(8,128)(2,1)} %get-tuple-element.67), channel_id=1, source_target_pairs={{0,6},{1,7},{2,0},{3,1},{4,2},{5,3},{6,4},{7,5},{8,14},{9,15},{10,... | collective-permute-start | bytes 1920008 | tf_op jit(solution)/shard_map/ppermute | solution.py:329
  615.8 49.9 %collective-permute-start.54 = (bf16[200,1600]{1,0:T(8,128)(2,1)}, bf16[200,1600]{1,0:T(8,128)(2,1)}, u32[]{:S(2)}, u32[]{:S(2)}) collective-permute-start(bf16[200,1600]{1,0:T(8,128)(2,1)} %get-tuple-element.69), channel_id=1, source_target_pairs={{0,4},{1,5},{2,6},{3,7},{4,0},{5,1},{6,2},{7,3},{8,12},{9,13},{10,... | collective-permute-start | bytes 1920008 | tf_op jit(solution)/shard_map/ppermute | solution.py:329
  624.6 78.1 %collective-permute-start.55 = (bf16[200,1600]{1,0:T(8,128)(2,1)}, bf16[200,1600]{1,0:T(8,128)(2,1)}, u32[]{:S(2)}, u32[]{:S(2)}) collective-permute-start(bf16[200,1600]{1,0:T(8,128)(2,1)} %get-tuple-element.68), channel_id=1, source_target_pairs={{0,2},{1,3},{2,4},{3,5},{4,6},{5,7},{6,0},{7,1},{8,10},{9,11},{10,... | collective-permute-start | bytes 1920008 | tf_op jit(solution)/shard_map/ppermute | solution.py:329
  663.8 73.3 %collective-permute-start.35 = (bf16[1024,896]{1,0:T(8,128)(2,1)S(1)}, bf16[1024,896]{1,0:T(8,128)(2,1)S(1)}, u32[]{:S(2)}, u32[]{:S(2)}) collective-permute-start(bf16[1024,896]{1,0:T(8,128)(2,1)S(1)} %convert_element_type.329), channel_id=1, source_target_pairs={{2,0},{3,1},{6,4},{7,5},{10,8},{11,9},{14,12},{15,13},{18,16},{19,... | collective-permute-start | bytes 5505032 | tf_op jit(solution)/shard_map/ppermute | solution.py:329
  665.5 68.4 %collective-permute-start.49 = (bf16[200,1600]{1,0:T(8,128)(2,1)S(1)}, bf16[200,1600]{1,0:T(8,128)(2,1)S(1)}, u32[]{:S(2)}, u32[]{:S(2)}) collective-permute-start(bf16[200,1600]{1,0:T(8,128)(2,1)S(1)} %get-tuple-element.70), channel_id=1, source_target_pairs={{0,6},{1,7},{2,0},{3,1},{4,2},{5,3},{6,4},{7,5},{8,14},{9,15},{10,... | collective-permute-start | bytes 1920008 | tf_op jit(solution)/shard_map/ppermute | solution.py:329
  665.6 69.0 %collective-permute-start.50 = (bf16[200,1600]{1,0:T(8,128)(2,1)S(1)}, bf16[200,1600]{1,0:T(8,128)(2,1)S(1)}, u32[]{:S(2)}, u32[]{:S(2)}) collective-permute-start(bf16[200,1600]{1,0:T(8,128)(2,1)S(1)} %get-tuple-element.72), channel_id=1, source_target_pairs={{0,4},{1,5},{2,6},{3,7},{4,0},{5,1},{6,2},{7,3},{8,12},{9,13},{10,... | collective-permute-start | bytes 1920008 | tf_op jit(solution)/shard_map/ppermute | solution.py:329
  665.7 68.9 %collective-permute-start.51 = (bf16[200,1600]{1,0:T(8,128)(2,1)S(1)}, bf16[200,1600]{1,0:T(8,128)(2,1)S(1)}, u32[]{:S(2)}, u32[]{:S(2)}) collective-permute-start(bf16[200,1600]{1,0:T(8,128)(2,1)S(1)} %get-tuple-element.71), channel_id=1, source_target_pairs={{0,2},{1,3},{2,4},{3,5},{4,6},{5,7},{6,0},{7,1},{8,10},{9,11},{10,... | collective-permute-start | bytes 1920008 | tf_op jit(solution)/shard_map/ppermute | solution.py:329
  702.7 52.3 %collective-permute-start.42 = (bf16[2,448,1600]{2,1,0:T(8,128)(2,1)}, bf16[2,448,1600]{2,1,0:T(8,128)(2,1)}, u32[]{:S(2)}, u32[]{:S(2)}) collective-permute-start(bf16[2,448,1600]{2,1,0:T(8,128)(2,1)} %fusion.14), channel_id=1, source_target_pairs={{0,8},{1,9},{2,10},{3,11},{4,12},{5,13},{6,14},{7,15},{8,0},{9,1},... | collective-permute-start | bytes 8601608 | tf_op jit(solution)/shard_map/ppermute | solution.py:329
  753.1 51.3 %collective-permute-start.38 = (bf16[672,1600]{1,0:T(8,128)(2,1)}, bf16[672,1600]{1,0:T(8,128)(2,1)}, u32[]{:S(2)}, u32[]{:S(2)}) collective-permute-start(bf16[672,1600]{1,0:T(8,128)(2,1)} %convolution_convert_fusion.2), channel_id=1, source_target_pairs={{0,16},{1,17},{2,18},{3,19},{4,20},{5,21},{6,22},{7,23},{8,24},{9,... | collective-permute-start | bytes 6451208 | tf_op jit(solution)/shard_map/ppermute | solution.py:329
  757.5 70.5 %collective-permute-start.43 = (bf16[448,1600]{1,0:T(8,128)(2,1)S(1)}, bf16[448,1600]{1,0:T(8,128)(2,1)S(1)}, u32[]{:S(2)}, u32[]{:S(2)}) collective-permute-start(bf16[448,1600]{1,0:T(8,128)(2,1)S(1)} %fusion.51), channel_id=1, source_target_pairs={{0,1},{1,0},{2,3},{3,2},{4,5},{5,4},{6,7},{7,6},{8,9},{9,8},{10,11... | collective-permute-start | bytes 4300808 | tf_op jit(solution)/shard_map/ppermute | solution.py:329
  762.2 66.6 %collective-permute-start.37 = (bf16[256,1600]{0,1:T(8,128)(2,1)S(1)}, bf16[256,1600]{0,1:T(8,128)(2,1)S(1)}, u32[]{:S(2)}, u32[]{:S(2)}) collective-permute-start(bf16[256,1600]{0,1:T(8,128)(2,1)S(1)} %fusion.67), channel_id=1, source_target_pairs={{0,1},{1,0},{2,3},{3,2},{4,5},{5,4},{6,7},{7,6},{8,9},{9,8},{10,11... | collective-permute-start | bytes 2457608 | tf_op jit(solution)/shard_map/ppermute | solution.py:329
  810.4 55.5 %collective-permute-start.40 = (bf16[168,1600]{1,0:T(8,128)(2,1)}, bf16[168,1600]{1,0:T(8,128)(2,1)}, u32[]{:S(2)}, u32[]{:S(2)}) collective-permute-start(bf16[168,1600]{1,0:T(8,128)(2,1)} %get-tuple-element.56), channel_id=1, source_target_pairs={{0,4},{1,5},{2,6},{3,7},{4,0},{5,1},{6,2},{7,3},{8,12},{9,13},{10,... | collective-permute-start | bytes 1612808 | tf_op jit(solution)/shard_map/ppermute | solution.py:329
  827.8 57.2 %collective-permute-start.41 = (bf16[168,1600]{1,0:T(8,128)(2,1)}, bf16[168,1600]{1,0:T(8,128)(2,1)}, u32[]{:S(2)}, u32[]{:S(2)}) collective-permute-start(bf16[168,1600]{1,0:T(8,128)(2,1)} %get-tuple-element.55), channel_id=1, source_target_pairs={{0,6},{1,7},{2,0},{3,1},{4,2},{5,3},{6,4},{7,5},{8,14},{9,15},{10,... | collective-permute-start | bytes 1612808 | tf_op jit(solution)/shard_map/ppermute | solution.py:329
  (119 other events, 2168.7 us)
Sparse Core Ops, SparseCore 0:
  832.1 173.0 all-reduce.6
